TPU v7x, 256 devices: a whole 4x4x8 slice. The times are simulated.
256 devices in a mesh: rad: 64 (over y, z, core), ell: 4 (over x).
Axes of the slice: x: 4, y: 4, z: 8, core: 2. Of those that a mesh axis runs over, the one named last changes fastest.
Arguments:
- field: bfloat16 [512, 128, 512], P('rad', 'ell'), may hold values from -6 to 6
- projection: bfloat16 [512, 128, 256], P('rad', 'ell'), may hold values from -0.75 to 0.75
- ell_ids: int32 [128], P('ell'), may hold values from 0 to 255, as said below
Outputs:
- share: float32 [128, 256], P('ell', 'rad')
- crest: float32 [128, 256], P('ell', 'rad')
Inputs may be any that keep to these rules, and one draw needn't show every extreme that they name: `ell_ids`: distinct and ascending.
All inputs are finite; a program needn't handle non-finite values.
Results may differ from a plain program's by a relative error of at most 0.0003.
Values may be sent and summed in bfloat16 or wider, within the bound.
No kernel may reach another device: no remote copies, remote signals or barrier semaphores. Data moves between devices by JAX's collectives and lax.ppermute only.
A program may use at most 64 MiB of HBM per device.

v0:
```python
import jax
import jax.numpy as jnp
from jax import lax
from jax.sharding import PartitionSpec as P


def side_by_side(arrays, axis, split_dim, concat_dim, along):
    widths = [a.shape[along] for a in arrays]
    both = jnp.concatenate(arrays, axis=along)
    result = lax.all_to_all(both, axis, split_axis=split_dim, concat_axis=concat_dim, tiled=True)
    return tuple(jnp.split(result, [sum(widths[:k]) for k in range(1, len(widths))], axis=along))


def gathered_once(shard, axis):
    leaves = jax.tree.leaves(shard)
    turns = sorted(range(len(leaves)), key=lambda k: -leaves[k].size)
    width = (1, *leaves[turns[0]].shape)[-1]
    lines = [
        jnp.pad(leaves[k].reshape(-1), (0, -leaves[k].size % width)).reshape(-1, width)
        for k in turns
    ]
    both, at, found = (lax.all_gather(jnp.concatenate(lines), axis), 0, {})
    for k, line in zip(turns, lines):
        piece = both[:, at : at + len(line)].reshape(len(both), -1)
        found[k] = piece[:, : leaves[k].size].reshape(-1, *leaves[k].shape)
        at += len(line)
    numbers = iter(range(len(leaves)))
    return jax.tree.map(lambda _: found[next(numbers)], shard)


def joined(shard, axis, combine):
    everything = gathered_once(shard, axis)
    first = jax.tree.map(lambda part: part[0], everything)

    def step(k, so_far):
        return combine(so_far, jax.tree.map(lambda part: part[k], everything))

    return lax.fori_loop(1, lax.axis_size(axis), step, first)


def combine_pair(first, second):
    return (first[0] + second[0], jnp.maximum(first[1], second[1]))


def per_device(field, projection, ell_ids):
    exchanged = lax.all_to_all(field, "rad", split_axis=2, concat_axis=0, tiled=True)
    slot_share = exchanged.shape[2]
    coef = jnp.einsum(
        "rem,ren->emn",
        exchanged,
        lax.all_gather(projection, "rad", axis=0, tiled=True),
        preferred_element_type=jnp.float32,
    )
    slots = lax.axis_index("rad") * slot_share + jnp.arange(slot_share, dtype=jnp.int32)
    valid = (slots[None, :] < 2 * ell_ids[:, None] + 1).astype(jnp.float32)
    energy_part = jnp.sum(valid[:, :, None] * coef * coef, axis=1)
    peak_part = jnp.max(valid[:, :, None] * jnp.abs(coef), axis=1)
    energy_all, peak_all = side_by_side((energy_part[None], peak_part[None]), "rad", 2, 0, 1)
    energy = jnp.sum(energy_all, axis=0)
    peak = jnp.max(peak_all, axis=0)
    local_sum = jnp.sum(energy, axis=0)
    local_top = jnp.max(peak, axis=0)
    column, top = joined((local_sum, local_top), "ell", combine_pair)
    column = column + 1e-06
    top = top + 1e-06
    total_ells = ell_ids.shape[0] * lax.axis_size("ell")
    share = total_ells * energy / column[None, :]
    crest = peak / top[None, :]
    return (share, crest)


def solution(mesh):
    in_specs = (P("rad", "ell", None), P("rad", "ell", None), P("ell"))
    out_specs = (P("ell", "rad"), P("ell", "rad"))
    return jax.shard_map(
        per_device, mesh=mesh, in_specs=in_specs, out_specs=out_specs, check_vma=False
    )
```

profile of v0, /device:TPU:1, one launch (start us, length us, event | category | flops | bytes accessed | tf_op | source)
XLA Modules:
  0.0 143.3 jit_solution(15682687795597710683)
XLA Ops:
  7.2 1.6 %copy.21 = bf16[8,32,256]{2,0,1:T(8,128)(2,1)} copy(bf16[8,32,256]{2,1,0:T(8,128)(2,1)} %param.6) | data formatting | bytes 262144 | tf_op args[1]
  8.9 1.7 %copy.18 = bf16[8,32,512]{1,0,2:T(8,128)(2,1)S(1)} copy(bf16[8,32,512]{2,1,0:T(8,128)(2,1)} %param.5) | data formatting | bytes 524288 | tf_op args[0]
  10.6 1.7 %reshape.65 = bf16[64,2,1024]{2,1,0:T(2,128)(2,1)} reshape(bf16[512,8,32]{2,1,0:T(8,128)(2,1)S(1)} %bitcast.33) | data formatting | bytes 524288
  12.3 13.1 %all-to-all-start = ((bf16[64,2,1024]{2,1,0:T(2,128)(2,1)}), bf16[64,2,1024]{2,1,0:T(2,128)(2,1)S(1)}, u32[]{:S(2)}, u32[]{:S(2)}) async-start(bf16[64,2,1024]{2,1,0:T(2,128)(2,1)} %reshape.65), calls=%async_computation | async-start | bytes 524288 | tf_op jit(solution)/shard_map/all_to_all | solution.py:46
  25.5 0.7 multiply_add_fusion
  26.1 0.1 compare_convert_fusion
  26.2 0.1 copy.17
  26.3 11.8 %all-to-all-done = bf16[64,2,1024]{2,1,0:T(2,128)(2,1)S(1)} async-done(((bf16[64,2,1024]{2,1,0:T(2,128)(2,1)}), bf16[64,2,1024]{2,1,0:T(2,128)(2,1)S(1)}, u32[]{:S(2)}, u32[]{:S(2)}) %all-to-all-start) | async-done | bytes 262176 | tf_op jit(solution)/shard_map/all_to_all | solution.py:46
  38.1 0.5 reshape.66
  38.6 0.3 copy.20
  38.9 1.0 copy.22
  39.9 61.6 %all-gather.4.cloned.1.call-done = bf16[512,32,256]{2,0,1:T(8,128)(2,1)} async-done(((bf16[8,32,256]{2,0,1:T(8,128)(2,1)}), bf16[512,32,256]{2,0,1:T(8,128)(2,1)}) %all-gather.4.cloned.1.call-update) | async-done | bytes 8388624 | tf_op jit(solution)/shard_map/all_gather | solution.py:51
  101.5 4.6 %fusion = (f32[32,256]{1,0:T(8,128)S(1)}, f32[32,256]{1,0:T(8,128)S(1)}) fusion(f32[32,8]{1,0:T(8,128)S(1)} %copy.17, bf16[512,32,8]{0,2,1:T(8,128)(2,1)S(1)} %copy.22, bf16[512,32,256]{2,0,1:T(8,128)(2,1)} %all-gather.4.cloned.1.call-done), kind=kOutput, calls=%fused_computation.3 | convolution fusion | flops 67485696 | bytes 8717312 | tf_op jit(solution)/shard_map/rem,ren->emn/dot_general | solution.py:48
  106.1 0.1 copy.23
  106.2 0.5 broadcast.33
  106.7 1.0 reduce.2
  107.7 0.1 reshape.67
  107.8 18.9 %all_to_all.36 = f32[64,1,256]{2,1,0:T(1,128)S(1)} all-to-all(f32[64,1,256]{2,1,0:T(1,128)S(1)} %reshape.67), channel_id=1, replica_groups=mesh['rad'=64,'ell'=4] {'rad'}, dimensions={0} | all-to-all | bytes 131072 | tf_op jit(solution)/shard_map/all_to_all | solution.py:10
  126.8 0.8 reduce.3
  127.6 0.2 reshape.68
  127.7 0.2 slice_reduce_fusion
  128.0 7.6 %all-gather.1 = f32[4,2,4]{2,1,0:T(2,128)S(1)} all-gather(f32[1,2,4]{2,1,0:T(2,128)S(1)} %maximum_bitcast_fusion), channel_id=2, replica_groups=mesh['rad'=64,'ell'=4] {'ell'}, dimensions={0}, use_global_device_ids=true | all-gather | bytes 160 | tf_op jit(solution)/shard_map/all_gather | solution.py:22
  135.7 0.1 while.17
  135.8 0.7 multiply_divide_fusion
  (12 shorter events, 0.1 us)
Async XLA Ops:
  7.2 94.3 %all-gather.4.cloned.1.call-start = ((), (), s32[]{:S(2)}) async-start(), calls=%async_computation.2 | async-start | bytes 8519680 | tf_op jit(solution)/shard_map/all_gather | solution.py:51
  12.3 25.8 %all-to-all-start = ((bf16[64,2,1024]{2,1,0:T(2,128)(2,1)}), bf16[64,2,1024]{2,1,0:T(2,128)(2,1)S(1)}, u32[]{:S(2)}, u32[]{:S(2)}) async-start(bf16[64,2,1024]{2,1,0:T(2,128)(2,1)} %reshape.65), calls=%async_computation | async-start | bytes 524288 | tf_op jit(solution)/shard_map/all_to_all | solution.py:46
Sparse Core Ops, SparseCore 0:
  10.5 90.9 all-gather.3
where the time goes:
time: 144 us; the launch traced here: 143 us
  waiting for transfers between devices  73.5 us (51%)
  blocking collectives  26.6 us (18%)
  between operations  14.2 us (10%)
  starting transfers between devices  13.2 us (9%)
  local copies, waits for them, and re-layouts  7.77 us (5%)
  matrix products  4.6 us (3%)
  other arithmetic  3.49 us (2%)
    all_gather x1, waiting for transfers between devices, per_device(): lax.all_gather(projection, 'rad', axis=0, tiled=True)  61.6 us
    all_to_all x1, blocking collectives, side_by_side(): lax.all_to_all(both, axis, split_axis=split_dim, concat_axis=concat_dim,...  18.9 us
    all_to_all x1, starting transfers between devices, per_device(): lax.all_to_all(field, 'rad', split_axis=2, concat_axis=0, tiled=True)  13.1 us
    all_to_all x1, waiting for transfers between devices, per_device(): lax.all_to_all(field, 'rad', split_axis=2, concat_axis=0, tiled=True)  11.8 us
    all_gather x1, blocking collectives, gathered_once(): both, at, found = (lax.all_gather(jnp.concatenate(lines), axis), 0, {})  7.65 us
    unnamed x7, local copies, waits for them, and re-layouts  6.35 us
    dot_general x1, matrix products, per_device(): jnp.einsum('rem,ren->emn', exchanged, lax.all_gather(projection, 'rad', a...  4.6 us
  transfers between devices with their start and end apart: 2, of which 2 were waited for; matrix products, arithmetic and copies ran while one was open for 4% of the time, Pallas kernels for 0%

commit v1 on v0

v1 whole, which is shorter than its diff:
```python
import jax
import jax.numpy as jnp
from jax import lax
from jax.sharding import PartitionSpec as P


def per_device(field, projection, ell_ids):
    radii, ells, slots = field.shape
    modes = projection.shape[2]
    owners = lax.axis_size("rad")
    parts = owners // ells
    groups = lax.axis_size("ell")
    width = slots // parts
    me = lax.axis_index("rad")
    turned = field.reshape(radii, ells, parts, width).transpose(1, 2, 0, 3)
    shared = jnp.broadcast_to(
        projection.transpose(1, 0, 2)[:, None], (ells, parts, radii, modes)
    )
    sent = jnp.concatenate([turned, shared], axis=-1).reshape(owners, radii, width + modes)
    got = lax.all_to_all(sent, "rad", 0, 0, tiled=True).reshape(owners * radii, width + modes)
    coef = lax.dot_general(
        got[:, :width],
        got[:, width:],
        (((0,), (0,)), ((), ())),
        preferred_element_type=jnp.float32,
    )
    ell = lax.dynamic_index_in_dim(ell_ids, me // parts, keepdims=False)
    slot = (me % parts) * width + jnp.arange(width, dtype=jnp.int32)
    valid = (slot < 2 * ell + 1).astype(jnp.float32)[:, None]
    energy_part = jnp.sum(valid * coef * coef, axis=0)
    peak_part = jnp.max(valid * jnp.abs(coef), axis=0)
    own = modes // owners
    both = jnp.concatenate(
        [energy_part.reshape(owners, own), peak_part.reshape(owners, own)], axis=-1
    )
    both = jnp.broadcast_to(both[:, None], (owners, groups, 2 * own))
    both = both.reshape(owners * groups, 2 * own)
    spread = lax.all_to_all(both, ("rad", "ell"), 0, 0, tiled=True)
    spread = spread.reshape(ells, parts, groups, 2 * own)
    energy = jnp.sum(spread[..., :own], axis=1)
    peak = jnp.max(spread[..., own:], axis=1)
    column = jnp.sum(energy, axis=(0, 1)) + 1e-06
    top = jnp.max(peak, axis=(0, 1)) + 1e-06
    group = lax.axis_index("ell")
    energy = lax.dynamic_index_in_dim(energy, group, axis=1, keepdims=False)
    peak = lax.dynamic_index_in_dim(peak, group, axis=1, keepdims=False)
    share = ells * groups * energy / column[None, :]
    crest = peak / top[None, :]
    return (share, crest)


def solution(mesh):
    in_specs = (P("rad", "ell", None), P("rad", "ell", None), P("ell"))
    out_specs = (P("ell", "rad"), P("ell", "rad"))
    return jax.shard_map(
        per_device, mesh=mesh, in_specs=in_specs, out_specs=out_specs, check_vma=False
    )
```

time: 144 us -> 58 us (0.40)
  waiting for transfers between devices: 73.5 us -> 28.1 us
  blocking collectives: 26.6 us -> 0 us
  between operations: 14.2 us -> 1.41 us
  starting transfers between devices: 13.2 us -> 21.9 us
  matrix products: 4.6 us -> 0.29 us
  local copies, waits for them, and re-layouts: 7.77 us -> 3.63 us
    all_gather x1 -> x0, waiting for transfers between devices: 61.6 us -> none  [per_device(): lax.all_gather(projection, 'rad', axis=0, tiled=True)]
    all_to_all x1 -> x0, blocking collectives: 18.9 us -> none  [side_by_side(): lax.all_to_all(both, axis, split_axis=split_dim, concat_axis=concat_dim,...]
    all_to_all x1 -> x2, waiting for transfers between devices: 11.8 us -> 28.1 us  [the longest x1 15.4 us: per_device(): lax.all_to_all(sent, 'rad', 0, 0, tiled=True)]
    all_to_all x1 -> x2, starting transfers between devices: 13.1 us -> 21.9 us  [the longest x1 13.1 us: per_device(): lax.all_to_all(sent, 'rad', 0, 0, tiled=True)]
    all_gather x1 -> x0, blocking collectives: 7.65 us -> none  [gathered_once(): both, at, found = (lax.all_gather(jnp.concatenate(lines), axis), 0, {})]
    unnamed x7 -> x5, local copies, waits for them, and re-layouts: 6.35 us -> 0.73 us
    dot_general x1, matrix products: 4.6 us -> 0.29 us  [per_device(): lax.dot_general(got[:, :width], got[:, width:], (((0,), (0,)), ((), ())),...]
  transfers between devices with their start and end apart: 2 -> 2, of which waited for: 2 -> 2; matrix products, arithmetic and copies ran while one was open for 4% -> 1% of each run, Pallas kernels for 0% -> 0%
where the time goes in v1:
time: 58 us; the launch traced here: 57.8 us
  waiting for transfers between devices  28.1 us (48%)
  starting transfers between devices  21.9 us (38%)
  local copies, waits for them, and re-layouts  3.63 us (6%)
  other arithmetic  2.43 us (4%)
  between operations  1.41 us (2%)
    all_to_all x1, waiting for transfers between devices, per_device(): lax.all_to_all(sent, 'rad', 0, 0, tiled=True)  15.4 us
    all_to_all x1, starting transfers between devices, per_device(): lax.all_to_all(sent, 'rad', 0, 0, tiled=True)  13.1 us
    all_to_all x1, waiting for transfers between devices, per_device(): spread = lax.all_to_all(both, ('rad', 'ell'), 0, 0, tiled=True)  12.7 us
    all_to_all x1, starting transfers between devices, per_device(): spread = lax.all_to_all(both, ('rad', 'ell'), 0, 0, tiled=True)  8.79 us
  transfers between devices with their start and end apart: 2, of which 2 were waited for; matrix products, arithmetic and copies ran while one was open for 1% of the time, Pallas kernels for 0%

profile of v1, /device:TPU:1, one launch (start us, length us, event | category | flops | bytes accessed | tf_op | source)
XLA Modules:
  0.0 57.8 jit_solution(18084630750400126629)
XLA Ops:
  0.6 0.0 copy-start
  0.6 1.0 %copy.24 = bf16[32,8,256]{2,1,0:T(8,128)(2,1)S(1)} copy(bf16[32,8,256]{2,0,1:T(8,128)(2,1)} %bitcast.16) | data formatting | bytes 262144 | tf_op jit(solution)/shard_map/transpose | solution.py:17
  1.7 0.0 copy-done
  1.7 0.1 reshape.47
  1.7 0.2 copy.29
  2.0 0.9 %pad_maximum_fusion = bf16[32,2,8,512]{3,2,1,0:T(8,128)(2,1)} fusion(bf16[32,2,8,256]{3,2,1,0:T(8,128)(2,1)S(1)} %broadcast_in_dim.4, bf16[32,2,8,256]{3,2,1,0:T(8,128)(2,1)S(1)} %bitcast.14), kind=kLoop, calls=%fused_computation | loop fusion | flops 1048576 | bytes 1048576 | tf_op jit(solution)/shard_map/concatenate | solution.py:19
  2.9 13.1 %all-to-all-start = ((bf16[64,8,512]{2,1,0:T(8,128)(2,1)}), bf16[64,8,512]{2,1,0:T(8,128)(2,1)S(1)}, u32[]{:S(2)}, u32[]{:S(2)}) async-start(bf16[64,8,512]{2,1,0:T(8,128)(2,1)} %bitcast.3), calls=%async_computation | async-start | bytes 1048576 | tf_op jit(solution)/shard_map/all_to_all | solution.py:20
  16.0 0.0 copy-start.1
  16.0 0.6 %copy-done.1 = s32[32]{0:T(128)S(1)} copy-done((s32[32]{0:T(128)S(1)}, s32[32]{0:T(128)}, u32[]{:S(2)}) %copy-start.1) | copy-done | bytes 152
  16.7 0.6 %dynamic_slice.11 = s32[1]{0:T(128)} dynamic-slice(s32[32]{0:T(128)S(1)} %copy-done.1, s32[]{:T(128)S(6)} %select_n.22), dynamic_slice_sizes={1} | dynamic-slice | bytes 12 | tf_op jit(solution)/shard_map/jit(dynamic_index_in_dim)/dynamic_slice | solution.py:27
  17.9 15.4 %all-to-all-done = bf16[64,8,512]{2,1,0:T(8,128)(2,1)S(1)} async-done(((bf16[64,8,512]{2,1,0:T(8,128)(2,1)}), bf16[64,8,512]{2,1,0:T(8,128)(2,1)S(1)}, u32[]{:S(2)}, u32[]{:S(2)}) %all-to-all-start) | async-done | bytes 524320 | tf_op jit(solution)/shard_map/all_to_all | solution.py:20
  33.3 0.3 fusion
  33.6 0.1 reshape.50
  33.7 0.1 reshape.51
  33.8 0.1 pad_maximum_fusion.1
  33.9 0.7 %broadcast_in_dim.5 = f32[64,4,8]{2,1,0:T(4,128)} broadcast(f32[64,8]{1,0:T(8,128)S(1)} %pad_maximum_fusion.1), dimensions={0,2} | broadcast | bytes 10240 | tf_op jit(solution)/shard_map/broadcast_in_dim | solution.py:36
  34.6 8.8 %all-to-all-start.1 = ((f32[256,1,8]{2,1,0:T(1,128)}), f32[256,1,8]{2,1,0:T(1,128)S(1)}, u32[]{:S(2)}, u32[]{:S(2)}) async-start(f32[256,1,8]{2,1,0:T(1,128)} %bitcast.5), calls=%async_computation.1 | async-start | bytes 262144 | tf_op jit(solution)/shard_map/all_to_all | solution.py:38
  43.4 12.7 %all-to-all-done.1 = f32[256,1,8]{2,1,0:T(1,128)S(1)} async-done(((f32[256,1,8]{2,1,0:T(1,128)}), f32[256,1,8]{2,1,0:T(1,128)S(1)}, u32[]{:S(2)}, u32[]{:S(2)}) %all-to-all-start.1) | async-done | bytes 8224 | tf_op jit(solution)/shard_map/all_to_all | solution.py:38
  56.1 0.2 slice_reduce_fusion
  56.3 0.1 copy.26
  56.4 0.1 copy.27
  56.5 0.7 %bitcast_divide_fusion = f32[32,4]{0,1:T(4,128)} fusion(f32[32,1,4]{0,2,1:T(4,128)S(1)} %copy.26, f32[4]{0:T(128)S(1)} %get-tuple-element.10), kind=kLoop, calls=%fused_computation.13 | loop fusion | flops 128 | bytes 1040 | tf_op jit(solution)/shard_map/div | solution.py:48
  57.1 0.7 %bitcast_divide_fusion.1 = f32[32,4]{0,1:T(4,128)} fusion(f32[32,1,4]{0,2,1:T(4,128)S(1)} %copy.27, f32[4]{0:T(128)S(1)} %get-tuple-element.11), kind=kLoop, calls=%fused_computation.14 | loop fusion | flops 256 | bytes 1040 | tf_op jit(solution)/shard_map/div | solution.py:47
  (4 shorter events, 0.1 us)
Async XLA Ops:
  0.6 1.0 %copy-start = (bf16[8,32,512]{2,1,0:T(8,128)(2,1)S(1)}, bf16[8,32,512]{2,1,0:T(8,128)(2,1)}, u32[]{:S(2)}) copy-start(bf16[8,32,512]{2,1,0:T(8,128)(2,1)} %param.3) | copy-start | bytes 786436
  2.9 30.4 %all-to-all-start = ((bf16[64,8,512]{2,1,0:T(8,128)(2,1)}), bf16[64,8,512]{2,1,0:T(8,128)(2,1)S(1)}, u32[]{:S(2)}, u32[]{:S(2)}) async-start(bf16[64,8,512]{2,1,0:T(8,128)(2,1)} %bitcast.3), calls=%async_computation | async-start | bytes 1048576 | tf_op jit(solution)/shard_map/all_to_all | solution.py:20
  16.0 0.7 %copy-start.1 = (s32[32]{0:T(128)S(1)}, s32[32]{0:T(128)}, u32[]{:S(2)}) copy-start(s32[32]{0:T(128)} %param.5) | copy-start | bytes 388
  34.6 21.5 %all-to-all-start.1 = ((f32[256,1,8]{2,1,0:T(1,128)}), f32[256,1,8]{2,1,0:T(1,128)S(1)}, u32[]{:S(2)}, u32[]{:S(2)}) async-start(f32[256,1,8]{2,1,0:T(1,128)} %bitcast.5), calls=%async_computation.1 | async-start | bytes 262144 | tf_op jit(solution)/shard_map/all_to_all | solution.py:38

commit v2 on v1

v2 whole, which is shorter than its diff:
```python
import jax
import jax.numpy as jnp
from jax import lax
from jax.sharding import Mesh
from jax.sharding import PartitionSpec as P

CORES = 2
CHIPS_Y = 4
CHIPS = ("y", "z")
WHERE = ("y", "z", "core")


def pick(modes, own, core):
    source = lax.broadcasted_iota(jnp.int32, (modes, modes // CORES), 0)
    target = lax.broadcasted_iota(jnp.int32, (modes, modes // CORES), 1)
    wanted = (target // own) * (own * CORES) + core * own + target % own
    return (source == wanted).astype(jnp.bfloat16)


def per_device(field, projection, ell_ids):
    radii, ells, slots = field.shape
    modes = projection.shape[2]
    groups = lax.axis_size("ell")
    own = modes // (ells * CORES)
    core = lax.axis_index("core")
    chip = lax.axis_index(CHIPS)
    group = lax.axis_index("ell")
    ell = lax.dynamic_index_in_dim(ell_ids, chip, keepdims=False)
    valid = (jnp.arange(slots, dtype=jnp.int32) < 2 * ell + 1).astype(jnp.float32)
    other = pick(modes, own, 1 - core)
    mine = pick(modes, own, core)
    sent = jnp.concatenate([field.transpose(1, 0, 2), projection.transpose(1, 0, 2)], axis=-1)
    sent, valid, other, mine, group = lax.optimization_barrier((sent, valid, other, mine, group))
    got = lax.all_to_all(sent, CHIPS, 0, 0, tiled=True).reshape(ells * radii, slots + modes)
    values, weights = got[:, :slots], got[:, slots:]

    def half(selection):
        chosen = lax.dot(weights, selection, preferred_element_type=jnp.float32)
        return lax.dot_general(
            values,
            chosen.astype(jnp.bfloat16),
            (((0,), (0,)), ((), ())),
            preferred_element_type=jnp.float32,
        )

    away = lax.ppermute(half(other), "core", [(0, 1), (1, 0)])
    coef = half(mine) + away
    energy = jnp.sum(valid[:, None] * coef * coef, axis=0)
    peak = jnp.max(valid[:, None] * jnp.abs(coef), axis=0)
    both = jnp.concatenate([energy.reshape(ells, own), peak.reshape(ells, own)], axis=-1)
    both = jnp.broadcast_to(both[:, None], (ells, groups, 2 * own))
    both = both.reshape(ells * groups, 2 * own)
    both, group = lax.optimization_barrier((both, group))
    spread = lax.all_to_all(both, (*CHIPS, "ell"), 0, 0, tiled=True)
    spread, group = lax.optimization_barrier((spread, group))
    spread = spread.reshape(ells, groups, 2 * own)
    column = jnp.sum(spread[..., :own], axis=(0, 1)) + 1e-06
    top = jnp.max(spread[..., own:], axis=(0, 1)) + 1e-06
    held = lax.dynamic_index_in_dim(spread, group, axis=1, keepdims=False)
    share = ells * groups * held[:, :own] / column[None, :]
    crest = held[:, own:] / top[None, :]
    return (share, crest)


def solution(mesh):
    devices = mesh.devices.reshape(CHIPS_Y, -1, CORES, mesh.shape["ell"])
    fine = Mesh(devices, ("y", "z", "core", "ell"))
    in_specs = (P(WHERE, "ell", None), P(WHERE, "ell", None), P("ell"))
    out_specs = (P("ell", WHERE), P("ell", WHERE))
    return jax.shard_map(
        per_device, mesh=fine, in_specs=in_specs, out_specs=out_specs, check_vma=False
    )
```

time: 58 us -> 54.2 us (0.934)
  blocking collectives: 0 us -> 43.2 us
  waiting for transfers between devices: 28.1 us -> 1.16 us
  starting transfers between devices: 21.9 us -> 3.78 us
  other arithmetic: 2.43 us -> 0.96 us
  local copies, waits for them, and re-layouts: 3.63 us -> 2.71 us
    all_to_all x0 -> x2, blocking collectives: none -> 43.2 us  [the longest x1 23.5 us: per_device(): lax.all_to_all(sent, CHIPS, 0, 0, tiled=True)]
    all_to_all x2 -> x0, waiting for transfers between devices: 28.1 us -> none  [the longest x1 15.4 us: per_device(): lax.all_to_all(sent, 'rad', 0, 0, tiled=True)]
    all_to_all x2 -> x0, starting transfers between devices: 21.9 us -> none  [the longest x1 13.1 us: per_device(): lax.all_to_all(sent, 'rad', 0, 0, tiled=True)]
    ppermute x0 -> x1, starting transfers between devices: none -> 3.78 us  [per_device(): away = lax.ppermute(half(other), 'core', [(0, 1), (1, 0)])]
    ppermute x0 -> x1, waiting for transfers between devices: none -> 1.16 us  [per_device(): away = lax.ppermute(half(other), 'core', [(0, 1), (1, 0)])]
    transpose x1 -> x0, local copies, waits for them, and re-layouts: 1.02 us -> none  [per_device(): projection.transpose(1, 0, 2)[:, None]]
    concatenate x2, other arithmetic: 0.93 us -> 0.1 us  [the longest x1 0.08 us: per_device(): jnp.concatenate([energy.reshape(ells, own), peak.reshape(ells, own)], axi...]
    broadcast_in_dim x2 -> x1, local copies, waits for them, and re-layouts: 0.68 us -> 0.02 us  [per_device(): both = jnp.broadcast_to(both[:, None], (ells, groups, 2 * own))]
  transfers between devices with their start and end apart: 2 -> 1, of which waited for: 2 -> 1; matrix products, arithmetic and copies ran while one was open for 1% -> 0% of each run, Pallas kernels for 0% -> 0%
where the time goes in v2:
time: 54.2 us; the launch traced here: 54 us
  blocking collectives  43.2 us (80%)
  starting transfers between devices  3.78 us (7%)
  local copies, waits for them, and re-layouts  2.71 us (5%)
  between operations  1.4 us (3%)
  waiting for transfers between devices  1.16 us (2%)
  other arithmetic  0.96 us (2%)
  matrix products  0.85 us (2%)
    all_to_all x1, blocking collectives, per_device(): lax.all_to_all(sent, CHIPS, 0, 0, tiled=True)  23.5 us
    all_to_all x1, blocking collectives, per_device(): spread = lax.all_to_all(both, (*CHIPS, 'ell'), 0, 0, tiled=True)  19.6 us
    ppermute x1, starting transfers between devices, per_device(): away = lax.ppermute(half(other), 'core', [(0, 1), (1, 0)])  3.78 us
    dynamic_slice x1, local copies, waits for them, and re-layouts, per_device(): ell = lax.dynamic_index_in_dim(ell_ids, chip, keepdims=False)  1.27 us
    ppermute x1, waiting for transfers between devices, per_device(): away = lax.ppermute(half(other), 'core', [(0, 1), (1, 0)])  1.16 us
    unnamed x4, local copies, waits for them, and re-layouts  1.14 us
  transfers between devices with their start and end apart: 1, of which 1 were waited for; matrix products, arithmetic and copies ran while one was open for 0% of the time, Pallas kernels for 0%

profile of v2, /device:TPU:1, one launch (start us, length us, event | category | flops | bytes accessed | tf_op | source)
XLA Modules:
  0.0 54.0 jit_solution(11499913575232177284)
XLA Ops:
  0.6 0.0 copy-start
  0.7 1.3 %dynamic_slice.8 = s32[1]{0:T(128)} dynamic-slice(s32[32]{0:T(128)} %param.5, s32[]{:T(128)S(6)} %select_n.27), dynamic_slice_sizes={1} | dynamic-slice | bytes 12 | tf_op jit(solution)/shard_map/jit(dynamic_index_in_dim)/dynamic_slice | solution.py:28
  2.6 1.0 %copy.22 = bf16[8,32,256]{2,0,1:T(8,128)(2,1)S(1)} copy(bf16[8,32,256]{2,1,0:T(8,128)(2,1)} %param.4) | data formatting | bytes 262144 | tf_op args[1]
  3.6 0.0 copy-done
  3.6 0.2 copy.21
  3.9 23.5 %all_to_all.17 = bf16[32,8,768]{2,1,0:T(8,128)(2,1)S(1)} all-to-all(bf16[32,8,768]{2,1,0:T(8,128)(2,1)S(1)} %pad_maximum_fusion), channel_id=1, replica_groups=mesh['y'=4,'z'=8,'core'=2,'ell'=4] {'y','z'}, dimensions={0} | all-to-all | bytes 786432 | tf_op jit(solution)/shard_map/all_to_all | solution.py:34
  27.4 0.4 fusion
  27.8 3.8 %collective-permute-start = (f32[512,128]{1,0:T(8,128)S(1)}, f32[512,128]{1,0:T(8,128)S(1)}, u32[]{:S(2)}, u32[]{:S(2)}) collective-permute-start(f32[512,128]{1,0:T(8,128)S(1)} %fusion), channel_id=1, source_target_pairs={{0,4},{4,0},{1,5},{5,1},{2,6},{6,2},{3,7},{7,3},{8,12},{12,8},{9,1... | collective-permute-start | bytes 786440 | tf_op jit(solution)/shard_map/ppermute | solution.py:46
  31.6 1.2 %collective-permute-done = f32[512,128]{1,0:T(8,128)S(1)} collective-permute-done((f32[512,128]{1,0:T(8,128)S(1)}, f32[512,128]{1,0:T(8,128)S(1)}, u32[]{:S(2)}, u32[]{:S(2)}) %collective-permute-start) | collective-permute-done | bytes 262176 | tf_op jit(solution)/shard_map/ppermute | solution.py:46
  32.8 0.4 fusion.1
  33.2 0.1 reshape.34
  33.3 0.1 reshape.35
  33.4 0.1 pad_maximum_fusion.1
  33.5 19.6 %all_to_all.18 = f32[128,1,8]{2,1,0:T(1,128)S(1)} all-to-all(f32[128,1,8]{2,1,0:T(1,128)S(1)} %bitcast.21), channel_id=1, replica_groups=mesh['y'=4,'z'=8,'core'=2,'ell'=4] {'y','z','ell'}, dimensions={0} | all-to-all | bytes 8192 | tf_op jit(solution)/shard_map/all_to_all | solution.py:54
  53.1 0.1 slice_reduce_fusion
  53.3 0.1 copy.18
  53.4 0.7 %slice_divide_fusion = (f32[32,4]{0,1:T(4,128)}, f32[32,4]{0,1:T(4,128)}) fusion(f32[32,8]{0,1:T(8,128)S(1)} %bitcast.22, f32[4]{0:T(128)S(1)} %broadcast_add_fusion, f32[4]{0:T(128)S(1)} %broadcast_add_fusion.1), kind=kLoop, calls=%fused_computation.24 | loop fusion | flops 384 | bytes 2080 | tf_op jit(solution)/shard_map/div | solution.py:61
  (10 shorter events, 0.1 us)
Async XLA Ops:
  0.6 3.0 %copy-start = (bf16[8,32,512]{2,1,0:T(8,128)(2,1)S(1)}, bf16[8,32,512]{2,1,0:T(8,128)(2,1)}, u32[]{:S(2)}) copy-start(bf16[8,32,512]{2,1,0:T(8,128)(2,1)} %param.3) | copy-start | bytes 786436
  27.8 4.9 %collective-permute-start = (f32[512,128]{1,0:T(8,128)S(1)}, f32[512,128]{1,0:T(8,128)S(1)}, u32[]{:S(2)}, u32[]{:S(2)}) collective-permute-start(f32[512,128]{1,0:T(8,128)S(1)} %fusion), channel_id=1, source_target_pairs={{0,4},{4,0},{1,5},{5,1},{2,6},{6,2},{3,7},{7,3},{8,12},{12,8},{9,1... | collective-permute-start | bytes 786440 | tf_op jit(solution)/shard_map/ppermute | solution.py:46

commit v3 on v2

--- a/solution.py
+++ b/solution.py
@@ -25,13 +25,13 @@
     core = lax.axis_index("core")
     chip = lax.axis_index(CHIPS)
     group = lax.axis_index("ell")
-    ell = lax.dynamic_index_in_dim(ell_ids, chip, keepdims=False)
-    valid = (jnp.arange(slots, dtype=jnp.int32) < 2 * ell + 1).astype(jnp.float32)
     other = pick(modes, own, 1 - core)
     mine = pick(modes, own, core)
     sent = jnp.concatenate([field.transpose(1, 0, 2), projection.transpose(1, 0, 2)], axis=-1)
-    sent, valid, other, mine, group = lax.optimization_barrier((sent, valid, other, mine, group))
-    got = lax.all_to_all(sent, CHIPS, 0, 0, tiled=True).reshape(ells * radii, slots + modes)
+    sent, other, mine, group, chip = lax.optimization_barrier((sent, other, mine, group, chip))
+    got = lax.all_to_all(sent, CHIPS, 0, 0, tiled=True)
+    got, chip = lax.optimization_barrier((got, chip))
+    got = got.reshape(ells * radii, slots + modes)
     values, weights = got[:, :slots], got[:, slots:]
 
     def half(selection):
@@ -43,8 +43,12 @@
             preferred_element_type=jnp.float32,
         )
 
-    away = lax.ppermute(half(other), "core", [(0, 1), (1, 0)])
-    coef = half(mine) + away
+    leaving, ell_ids, chip = lax.optimization_barrier((half(other), ell_ids, chip))
+    away = lax.ppermute(leaving, "core", [(0, 1), (1, 0)])
+    kept = lax.optimization_barrier(half(mine))
+    ell = lax.dynamic_index_in_dim(ell_ids, chip, keepdims=False)
+    valid = (jnp.arange(slots, dtype=jnp.int32) < 2 * ell + 1).astype(jnp.float32)
+    coef = kept + away
     energy = jnp.sum(valid[:, None] * coef * coef, axis=0)
     peak = jnp.max(valid[:, None] * jnp.abs(coef), axis=0)
     both = jnp.concatenate([energy.reshape(ells, own), peak.reshape(ells, own)], axis=-1)

time: 54.2 us -> 53.2 us (0.982)
  waiting for transfers between devices: 1.16 us -> 0.01 us
    ppermute x1, waiting for transfers between devices: 1.16 us -> 0.01 us  [per_device(): away = lax.ppermute(leaving, 'core', [(0, 1), (1, 0)])]
    dynamic_slice x1, local copies, waits for them, and re-layouts: 1.27 us -> 0.58 us  [per_device(): ell = lax.dynamic_index_in_dim(ell_ids, chip, keepdims=False)]
    unnamed x4 -> x6, local copies, waits for them, and re-layouts: 1.14 us -> 1.83 us
  transfers between devices with their start and end apart: 1 -> 1, of which waited for: 1 -> 0; matrix products, arithmetic and copies ran while one was open for 0% -> 2% of each run, Pallas kernels for 0% -> 0%
where the time goes in v3:
time: 53.2 us; the launch traced here: 53 us
  blocking collectives  43.2 us (81%)
  starting transfers between devices  3.78 us (7%)
  local copies, waits for them, and re-layouts  2.71 us (5%)
  between operations  1.44 us (3%)
  other arithmetic  1.11 us (2%)
  matrix products  0.82 us (2%)
    all_to_all x1, blocking collectives, per_device(): got = lax.all_to_all(sent, CHIPS, 0, 0, tiled=True)  23.5 us
    all_to_all x1, blocking collectives, per_device(): spread = lax.all_to_all(both, (*CHIPS, 'ell'), 0, 0, tiled=True)  19.6 us
    ppermute x1, starting transfers between devices, per_device(): away = lax.ppermute(leaving, 'core', [(0, 1), (1, 0)])  3.78 us
    unnamed x6, local copies, waits for them, and re-layouts  1.83 us
  transfers between devices with their start and end apart: 1, of which 0 were waited for; matrix products, arithmetic and copies ran while one was open for 2% of the time, Pallas kernels for 0%

profile of v3, /device:TPU:1, one launch (start us, length us, event | category | flops | bytes accessed | tf_op | source)
XLA Modules:
  0.0 53.0 jit_solution(7383780751252261892)
XLA Ops:
  0.6 0.0 copy-start
  0.7 1.0 %copy.22 = bf16[8,32,256]{2,0,1:T(8,128)(2,1)S(1)} copy(bf16[8,32,256]{2,1,0:T(8,128)(2,1)} %param.4) | data formatting | bytes 262144 | tf_op args[1]
  1.7 0.0 copy-done
  1.7 0.2 copy.21
  2.0 23.5 %all_to_all.17 = bf16[32,8,768]{2,1,0:T(8,128)(2,1)S(1)} all-to-all(bf16[32,8,768]{2,1,0:T(8,128)(2,1)S(1)} %pad_maximum_fusion), channel_id=1, replica_groups=mesh['y'=4,'z'=8,'core'=2,'ell'=4] {'y','z'}, dimensions={0} | all-to-all | bytes 786432 | tf_op jit(solution)/shard_map/all_to_all | solution.py:32
  25.5 0.4 fusion
  25.9 3.8 %collective-permute-start = (f32[512,128]{1,0:T(8,128)S(1)}, f32[512,128]{1,0:T(8,128)S(1)}, u32[]{:S(2)}, u32[]{:S(2)}) collective-permute-start(f32[512,128]{1,0:T(8,128)S(1)} %fusion), channel_id=1, source_target_pairs={{0,4},{4,0},{1,5},{5,1},{2,6},{6,2},{3,7},{7,3},{8,12},{12,8},{9,1... | collective-permute-start | bytes 786440 | tf_op jit(solution)/shard_map/ppermute | solution.py:47
  29.7 0.4 fusion.1
  30.1 0.0 copy-start.1
  30.1 0.7 %copy-done.1 = s32[32]{0:T(128)S(1)} copy-done((s32[32]{0:T(128)S(1)}, s32[32]{0:T(128)}, u32[]{:S(2)}) %copy-start.1) | copy-done | bytes 152
  30.8 0.6 %dynamic_slice.8 = s32[1]{0:T(128)} dynamic-slice(s32[32]{0:T(128)S(1)} %copy-done.1, s32[]{:T(128)S(6)} %select_n.29), dynamic_slice_sizes={1} | dynamic-slice | bytes 12 | tf_op jit(solution)/shard_map/jit(dynamic_index_in_dim)/dynamic_slice | solution.py:49
  32.0 0.0 collective-permute-done
  32.0 0.2 fusion.2
  32.2 0.1 reshape.38
  32.3 0.1 reshape.39
  32.4 0.1 pad_maximum_fusion.1
  32.5 19.6 %all_to_all.18 = f32[128,1,8]{2,1,0:T(1,128)S(1)} all-to-all(f32[128,1,8]{2,1,0:T(1,128)S(1)} %bitcast.21), channel_id=1, replica_groups=mesh['y'=4,'z'=8,'core'=2,'ell'=4] {'y','z','ell'}, dimensions={0} | all-to-all | bytes 8192 | tf_op jit(solution)/shard_map/all_to_all | solution.py:58
  52.1 0.1 slice_reduce_fusion
  52.3 0.1 copy.18
  52.4 0.7 %slice_divide_fusion = (f32[32,4]{0,1:T(4,128)}, f32[32,4]{0,1:T(4,128)}) fusion(f32[32,8]{0,1:T(8,128)S(1)} %bitcast.22, f32[4]{0:T(128)S(1)} %broadcast_add_fusion, f32[4]{0:T(128)S(1)} %broadcast_add_fusion.1), kind=kLoop, calls=%fused_computation.24 | loop fusion | flops 384 | bytes 2080 | tf_op jit(solution)/shard_map/div | solution.py:65
  (10 shorter events, 0.1 us)
Async XLA Ops:
  0.6 1.1 %copy-start = (bf16[8,32,512]{2,1,0:T(8,128)(2,1)S(1)}, bf16[8,32,512]{2,1,0:T(8,128)(2,1)}, u32[]{:S(2)}) copy-start(bf16[8,32,512]{2,1,0:T(8,128)(2,1)} %param.3) | copy-start | bytes 786436
  25.9 6.1 %collective-permute-start = (f32[512,128]{1,0:T(8,128)S(1)}, f32[512,128]{1,0:T(8,128)S(1)}, u32[]{:S(2)}, u32[]{:S(2)}) collective-permute-start(f32[512,128]{1,0:T(8,128)S(1)} %fusion), channel_id=1, source_target_pairs={{0,4},{4,0},{1,5},{5,1},{2,6},{6,2},{3,7},{7,3},{8,12},{12,8},{9,1... | collective-permute-start | bytes 786440 | tf_op jit(solution)/shard_map/ppermute | solution.py:47
  30.1 0.7 %copy-start.1 = (s32[32]{0:T(128)S(1)}, s32[32]{0:T(128)}, u32[]{:S(2)}) copy-start(s32[32]{0:T(128)} %param.5) | copy-start | bytes 388

commit v4 on v3

--- a/solution.py
+++ b/solution.py
@@ -28,7 +28,10 @@
     other = pick(modes, own, 1 - core)
     mine = pick(modes, own, core)
     sent = jnp.concatenate([field.transpose(1, 0, 2), projection.transpose(1, 0, 2)], axis=-1)
-    sent, other, mine, group, chip = lax.optimization_barrier((sent, other, mine, group, chip))
+    needed = (jnp.arange(slots, dtype=jnp.int32) + 1) // 2
+    sent, other, mine, needed, group, chip = lax.optimization_barrier(
+        (sent, other, mine, needed, group, chip)
+    )
     got = lax.all_to_all(sent, CHIPS, 0, 0, tiled=True)
     got, chip = lax.optimization_barrier((got, chip))
     got = got.reshape(ells * radii, slots + modes)
@@ -43,11 +46,12 @@
             preferred_element_type=jnp.float32,
         )
 
-    leaving, ell_ids, chip = lax.optimization_barrier((half(other), ell_ids, chip))
+    leaving, chip = lax.optimization_barrier((half(other), chip))
     away = lax.ppermute(leaving, "core", [(0, 1), (1, 0)])
     kept = lax.optimization_barrier(half(mine))
-    ell = lax.dynamic_index_in_dim(ell_ids, chip, keepdims=False)
-    valid = (jnp.arange(slots, dtype=jnp.int32) < 2 * ell + 1).astype(jnp.float32)
+    here = jnp.arange(ells, dtype=jnp.int32)[None, :] == chip
+    inside = needed[:, None] <= ell_ids[None, :]
+    valid = jnp.sum((here & inside).astype(jnp.float32), axis=1)
     coef = kept + away
     energy = jnp.sum(valid[:, None] * coef * coef, axis=0)
     peak = jnp.max(valid[:, None] * jnp.abs(coef), axis=0)

time: 53.2 us -> 52.1 us (0.979)
  between operations: 1.44 us -> 0.79 us
  local copies, waits for them, and re-layouts: 2.71 us -> 2.11 us
    dynamic_slice x1 -> x0, local copies, waits for them, and re-layouts: 0.58 us -> none  [per_device(): ell = lax.dynamic_index_in_dim(ell_ids, chip, keepdims=False)]
  transfers between devices with their start and end apart: 1 -> 1, of which waited for: 0 -> 0; matrix products, arithmetic and copies ran while one was open for 2% -> 1% of each run, Pallas kernels for 0% -> 0%
where the time goes in v4:
time: 52.1 us; the launch traced here: 51.9 us
  blocking collectives  43.2 us (83%)
  starting transfers between devices  3.78 us (7%)
  local copies, waits for them, and re-layouts  2.11 us (4%)
  other arithmetic  1.21 us (2%)
  matrix products  0.82 us (2%)
  between operations  0.79 us (2%)
    all_to_all x1, blocking collectives, per_device(): got = lax.all_to_all(sent, CHIPS, 0, 0, tiled=True)  23.5 us
    all_to_all x1, blocking collectives, per_device(): spread = lax.all_to_all(both, (*CHIPS, 'ell'), 0, 0, tiled=True)  19.6 us
    ppermute x1, starting transfers between devices, per_device(): away = lax.ppermute(leaving, 'core', [(0, 1), (1, 0)])  3.78 us
    unnamed x6, local copies, waits for them, and re-layouts  1.81 us
  transfers between devices with their start and end apart: 1, of which 0 were waited for; matrix products, arithmetic and copies ran while one was open for 1% of the time, Pallas kernels for 0%

profile of v4, /device:TPU:1, one launch (start us, length us, event | category | flops | bytes accessed | tf_op | source)
XLA Modules:
  0.0 51.9 jit_solution(17144679257664666011)
XLA Ops:
  0.6 0.0 copy-start
  0.7 1.0 %copy.22 = bf16[8,32,256]{2,0,1:T(8,128)(2,1)S(1)} copy(bf16[8,32,256]{2,1,0:T(8,128)(2,1)} %param.4) | data formatting | bytes 262144 | tf_op args[1]
  1.7 0.0 copy-done
  1.7 0.2 copy.21
  2.0 23.5 %all_to_all.17 = bf16[32,8,768]{2,1,0:T(8,128)(2,1)S(1)} all-to-all(bf16[32,8,768]{2,1,0:T(8,128)(2,1)S(1)} %pad_maximum_fusion), channel_id=1, replica_groups=mesh['y'=4,'z'=8,'core'=2,'ell'=4] {'y','z'}, dimensions={0} | all-to-all | bytes 786432 | tf_op jit(solution)/shard_map/all_to_all | solution.py:35
  25.5 0.4 fusion
  25.9 3.8 %collective-permute-start = (f32[512,128]{1,0:T(8,128)S(1)}, f32[512,128]{1,0:T(8,128)S(1)}, u32[]{:S(2)}, u32[]{:S(2)}) collective-permute-start(f32[512,128]{1,0:T(8,128)S(1)} %fusion), channel_id=1, source_target_pairs={{0,4},{4,0},{1,5},{5,1},{2,6},{6,2},{3,7},{7,3},{8,12},{12,8},{9,1... | collective-permute-start | bytes 786440 | tf_op jit(solution)/shard_map/ppermute | solution.py:50
  29.7 0.4 fusion.1
  30.1 0.0 copy-start.1
  30.2 0.6 %copy-done.1 = s32[32]{0:T(128)S(1)} copy-done((s32[32]{0:T(128)S(1)}, s32[32]{0:T(128)}, u32[]{:S(2)}) %copy-start.1) | copy-done | bytes 152
  30.8 0.1 convert_reduce_fusion
  30.9 0.0 collective-permute-done
  30.9 0.2 fusion.2
  31.0 0.1 reshape.38
  31.2 0.1 reshape.37
  31.3 0.1 pad_maximum_fusion.1
  31.4 19.6 %all_to_all.18 = f32[128,1,8]{2,1,0:T(1,128)S(1)} all-to-all(f32[128,1,8]{2,1,0:T(1,128)S(1)} %bitcast.20), channel_id=1, replica_groups=mesh['y'=4,'z'=8,'core'=2,'ell'=4] {'y','z','ell'}, dimensions={0} | all-to-all | bytes 8192 | tf_op jit(solution)/shard_map/all_to_all | solution.py:62
  51.0 0.1 slice_reduce_fusion
  51.1 0.1 copy.18
  51.2 0.7 %slice_divide_fusion = (f32[32,4]{0,1:T(4,128)}, f32[32,4]{0,1:T(4,128)}) fusion(f32[32,8]{0,1:T(8,128)S(1)} %bitcast.21, f32[4]{0:T(128)S(1)} %broadcast_add_fusion, f32[4]{0:T(128)S(1)} %broadcast_add_fusion.1), kind=kLoop, calls=%fused_computation.30 | loop fusion | flops 384 | bytes 2080 | tf_op jit(solution)/shard_map/div | solution.py:69
  (11 shorter events, 0.1 us)
Async XLA Ops:
  0.6 1.1 %copy-start = (bf16[8,32,512]{2,1,0:T(8,128)(2,1)S(1)}, bf16[8,32,512]{2,1,0:T(8,128)(2,1)}, u32[]{:S(2)}) copy-start(bf16[8,32,512]{2,1,0:T(8,128)(2,1)} %param.3) | copy-start | bytes 786436
  25.9 5.0 %collective-permute-start = (f32[512,128]{1,0:T(8,128)S(1)}, f32[512,128]{1,0:T(8,128)S(1)}, u32[]{:S(2)}, u32[]{:S(2)}) collective-permute-start(f32[512,128]{1,0:T(8,128)S(1)} %fusion), channel_id=1, source_target_pairs={{0,4},{4,0},{1,5},{5,1},{2,6},{6,2},{3,7},{7,3},{8,12},{12,8},{9,1... | collective-permute-start | bytes 786440 | tf_op jit(solution)/shard_map/ppermute | solution.py:50
  30.1 0.7 %copy-start.1 = (s32[32]{0:T(128)S(1)}, s32[32]{0:T(128)}, u32[]{:S(2)}) copy-start(s32[32]{0:T(128)} %param.5) | copy-start | bytes 388

commit v5 on v3

v5 whole, which is shorter than its diff:
```python
import functools

import jax
import jax.numpy as jnp
from jax import lax
from jax.experimental import pallas as pl
from jax.experimental.pallas import tpu as pltpu
from jax.sharding import Mesh
from jax.sharding import PartitionSpec as P

CORES = 2
CHIPS_Y = 4
SCOPED = 4 * 2**20
CHIPS = ("y", "z")
WHERE = ("y", "z", "core")


def pick(modes, own, core):
    source = lax.broadcasted_iota(jnp.int32, (modes, modes // CORES), 0)
    target = lax.broadcasted_iota(jnp.int32, (modes, modes // CORES), 1)
    wanted = (target // own) * (own * CORES) + core * own + target % own
    return (source == wanted).astype(jnp.bfloat16)


def spread_kernel(own, groups, kept, away, ids, out):
    coef = kept[...] + away[...]
    here = lax.broadcasted_iota(jnp.int32, ids.shape, 1) == lax.axis_index(CHIPS)
    ell = jnp.sum(jnp.where(here, ids[...], 0), axis=1, keepdims=True)
    slot = lax.broadcasted_iota(jnp.int32, coef.shape, 0)
    chosen = jnp.where(slot < 2 * ell + 1, coef, 0.0)
    energy = jnp.sum(chosen * coef, axis=0, keepdims=True)
    peak = jnp.max(jnp.abs(chosen), axis=0, keepdims=True)
    count = out.shape[0] // groups
    width = energy.shape[1]
    lane = lax.broadcasted_iota(jnp.int32, (count, width), 1)
    mine = lane // own == lax.broadcasted_iota(jnp.int32, (count, width), 0)
    energies = jnp.where(mine, energy, 0.0)
    peaks = jnp.where(mine, peak, 0.0)
    shift = own
    while shift < width:
        energies = energies + pltpu.roll(energies, shift, 1)
        peaks = peaks + pltpu.roll(peaks, shift, 1)
        shift *= 2
    rows = jnp.where(lane < own, energies, peaks)
    for group in range(groups):
        out[pl.ds(group * count, count)] = rows


def scale_kernel(own, ells, groups, spread, share, crest):
    values = spread[...]
    column = jnp.sum(values, axis=0, keepdims=True) + 1e-06
    top = jnp.max(values, axis=0, keepdims=True) + 1e-06
    first = pl.multiple_of(lax.axis_index("ell") * ells, ells)
    held = spread[pl.ds(first, ells)]
    lane = lax.broadcasted_iota(jnp.int32, held.shape, 1)
    scaled = jnp.where(lane < own, ells * groups * held / column, held / top)
    turned = scaled.T
    share[...] = turned[:own]
    crest[...] = turned[own : 2 * own]


def per_device(field, projection, ell_ids):
    radii, ells, slots = field.shape
    modes = projection.shape[2]
    groups = lax.axis_size("ell")
    own = modes // (ells * CORES)
    core = lax.axis_index("core")
    other = pick(modes, own, 1 - core)
    mine = pick(modes, own, core)
    sent = jnp.concatenate([field.transpose(1, 0, 2), projection.transpose(1, 0, 2)], axis=-1)
    sent, other, mine = lax.optimization_barrier((sent, other, mine))
    got = lax.all_to_all(sent, CHIPS, 0, 0, tiled=True)
    got, ell_ids = lax.optimization_barrier((got, ell_ids))
    got = got.reshape(ells * radii, slots + modes)
    values, weights = got[:, :slots], got[:, slots:]

    def half(selection):
        chosen = lax.dot(weights, selection, preferred_element_type=jnp.float32)
        return lax.dot_general(
            values,
            chosen.astype(jnp.bfloat16),
            (((0,), (0,)), ((), ())),
            preferred_element_type=jnp.float32,
        )

    away = lax.ppermute(half(other), "core", [(0, 1), (1, 0)])
    kept = lax.optimization_barrier(half(mine))
    both = pl.pallas_call(
        functools.partial(spread_kernel, own, groups),
        out_shape=jax.ShapeDtypeStruct((ells * groups, modes // CORES), jnp.float32),
        in_specs=[pl.BlockSpec(memory_space=pltpu.VMEM)] * 3,
        out_specs=pl.BlockSpec(memory_space=pltpu.VMEM),
        compiler_params=pltpu.CompilerParams(vmem_limit_bytes=SCOPED),
    )(kept, away, ell_ids[None])
    spread = lax.all_to_all(both, ("ell", *CHIPS), 0, 0, tiled=True)
    shape = jax.ShapeDtypeStruct((own, ells), jnp.float32)
    share, crest = pl.pallas_call(
        functools.partial(scale_kernel, own, ells, groups),
        out_shape=(shape, shape),
        in_specs=[pl.BlockSpec(memory_space=pltpu.VMEM)],
        out_specs=(pl.BlockSpec(memory_space=pltpu.VMEM),) * 2,
        compiler_params=pltpu.CompilerParams(vmem_limit_bytes=SCOPED),
    )(spread)
    return (share.T, crest.T)


def solution(mesh):
    devices = mesh.devices.reshape(CHIPS_Y, -1, CORES, mesh.shape["ell"])
    fine = Mesh(devices, ("y", "z", "core", "ell"))
    in_specs = (P(WHERE, "ell", None), P(WHERE, "ell", None), P("ell"))
    out_specs = (P("ell", WHERE), P("ell", WHERE))
    return jax.shard_map(
        per_device, mesh=fine, in_specs=in_specs, out_specs=out_specs, check_vma=False
    )
```

time: 53.2 us -> 51.9 us (0.976)
  local copies, waits for them, and re-layouts: 2.71 us -> 1.18 us
  Pallas kernels: 0 us -> 1.21 us
  other arithmetic: 1.11 us -> 0.09 us
  waiting for transfers between devices: 0.01 us -> 0.74 us
  between operations: 1.44 us -> 0.73 us
    pallas_call x0 -> x2, Pallas kernels: none -> 1.21 us  [the longest x1 0.68 us: per_device(): pl.pallas_call(functools.partial(scale_kernel, own, ells, groups), out_sh...]
    ppermute x1, waiting for transfers between devices: 0.01 us -> 0.74 us  [per_device(): away = lax.ppermute(half(other), 'core', [(0, 1), (1, 0)])]
    div x1 -> x0, other arithmetic: 0.66 us -> none  [per_device(): crest = held[:, own:] / top[None, :]]
    dynamic_slice x3 -> x0, local copies, waits for them, and re-layouts: 0.66 us -> none  [the longest x1 0.58 us: per_device(): ell = lax.dynamic_index_in_dim(ell_ids, chip, keepdims=False)]
    unnamed x6, local copies, waits for them, and re-layouts: 1.83 us -> 1.18 us
  transfers between devices with their start and end apart: 1 -> 1, of which waited for: 0 -> 1; matrix products, arithmetic and copies ran while one was open for 2% -> 1% of each run, Pallas kernels for 0% -> 0%
where the time goes in v5:
time: 51.9 us; the launch traced here: 51.7 us
  blocking collectives  43.2 us (83%)
  starting transfers between devices  3.78 us (7%)
  Pallas kernels  1.21 us (2%)
  local copies, waits for them, and re-layouts  1.18 us (2%)
  matrix products  0.81 us (2%)
  waiting for transfers between devices  0.74 us (1%)
  between operations  0.73 us (1%)
    all_to_all x1, blocking collectives, per_device(): got = lax.all_to_all(sent, CHIPS, 0, 0, tiled=True)  23.5 us
    all_to_all x1, blocking collectives, per_device(): spread = lax.all_to_all(both, ('ell', *CHIPS), 0, 0, tiled=True)  19.6 us
    ppermute x1, starting transfers between devices, per_device(): away = lax.ppermute(half(other), 'core', [(0, 1), (1, 0)])  3.78 us
    unnamed x6, local copies, waits for them, and re-layouts  1.18 us
  transfers between devices with their start and end apart: 1, of which 1 were waited for; matrix products, arithmetic and copies ran while one was open for 1% of the time, Pallas kernels for 0%

profile of v5, /device:TPU:1, one launch (start us, length us, event | category | flops | bytes accessed | tf_op | source)
XLA Modules:
  0.0 51.7 jit_solution(14517053583869879033)
XLA Ops:
  0.6 0.0 copy-start.1
  0.7 1.0 %copy.13 = bf16[8,32,256]{2,0,1:T(8,128)(2,1)S(1)} copy(bf16[8,32,256]{2,1,0:T(8,128)(2,1)} %param.4) | data formatting | bytes 262144 | tf_op args[1]
  1.7 0.0 copy-done.1
  1.7 0.2 copy.12
  2.0 23.5 %all_to_all.16 = bf16[32,8,768]{2,1,0:T(8,128)(2,1)S(1)} all-to-all(bf16[32,8,768]{2,1,0:T(8,128)(2,1)S(1)} %pad_maximum_fusion), channel_id=1, replica_groups=mesh['y'=4,'z'=8,'core'=2,'ell'=4] {'y','z'}, dimensions={0} | all-to-all | bytes 786432 | tf_op jit(solution)/shard_map/all_to_all | solution.py:72
  25.5 0.4 fusion.1
  25.9 3.8 %collective-permute-start = (f32[512,128]{1,0:T(8,128)S(1)}, f32[512,128]{1,0:T(8,128)S(1)}, u32[]{:S(2)}, u32[]{:S(2)}) collective-permute-start(f32[512,128]{1,0:T(8,128)S(1)} %fusion.1), channel_id=1, source_target_pairs={{0,4},{4,0},{1,5},{5,1},{2,6},{6,2},{3,7},{7,3},{8,12},{12,8},{9,1... | collective-permute-start | bytes 786440 | tf_op jit(solution)/shard_map/ppermute | solution.py:86
  29.7 0.4 fusion.kept
  30.1 0.0 copy-start
  30.1 0.7 %collective-permute-done.away = f32[512,128]{1,0:T(8,128)S(1)} collective-permute-done((f32[512,128]{1,0:T(8,128)S(1)}, f32[512,128]{1,0:T(8,128)S(1)}, u32[]{:S(2)}, u32[]{:S(2)}) %collective-permute-start) | collective-permute-done | bytes 262176 | tf_op jit(solution)/shard_map/ppermute | solution.py:86
  30.8 0.0 copy-done
  30.8 0.5 %shard_map.50 = f32[128,128]{1,0:T(8,128)S(1)} custom-call(f32[512,128]{1,0:T(8,128)S(1)} %fusion.kept, f32[512,128]{1,0:T(8,128)S(1)} %collective-permute-done.away, s32[1,32]{1,0:T(1,128)S(1)} %bitcast.18), custom_call_target="tpu_custom_call" | custom-call | tf_op jit(solution)/shard_map/pallas_call | solution.py:88
  31.4 19.6 %all_to_all.17 = f32[128,1,128]{2,1,0:T(1,128)S(1)} all-to-all(f32[128,1,128]{2,1,0:T(1,128)S(1)} %bitcast.17), channel_id=1, replica_groups=mesh['y'=4,'z'=8,'core'=2,'ell'=4] {'ell','y','z'}, dimensions={0} | all-to-all | bytes 131072 | tf_op jit(solution)/shard_map/all_to_all | solution.py:95
  51.0 0.7 %shard_map.51 = (f32[4,32]{1,0:T(4,128)}, f32[4,32]{1,0:T(4,128)}) custom-call(f32[128,128]{1,0:T(8,128)S(1)} %bitcast.16), custom_call_target="tpu_custom_call" | custom-call | tf_op jit(solution)/shard_map/pallas_call | solution.py:97
  (5 shorter events, 0.1 us)
Async XLA Ops:
  0.6 1.1 %copy-start.1 = (bf16[8,32,512]{2,1,0:T(8,128)(2,1)S(1)}, bf16[8,32,512]{2,1,0:T(8,128)(2,1)}, u32[]{:S(2)}) copy-start(bf16[8,32,512]{2,1,0:T(8,128)(2,1)} %param.3) | copy-start | bytes 786436
  25.9 4.9 %collective-permute-start = (f32[512,128]{1,0:T(8,128)S(1)}, f32[512,128]{1,0:T(8,128)S(1)}, u32[]{:S(2)}, u32[]{:S(2)}) collective-permute-start(f32[512,128]{1,0:T(8,128)S(1)} %fusion.1), channel_id=1, source_target_pairs={{0,4},{4,0},{1,5},{5,1},{2,6},{6,2},{3,7},{7,3},{8,12},{12,8},{9,1... | collective-permute-start | bytes 786440 | tf_op jit(solution)/shard_map/ppermute | solution.py:86
  30.1 0.8 %copy-start = (s32[32]{0:T(128)S(1)}, s32[32]{0:T(128)}, u32[]{:S(2)}) copy-start(s32[32]{0:T(128)} %param.5) | copy-start | bytes 388

commit v6 on v5

--- a/solution.py
+++ b/solution.py
@@ -22,7 +22,7 @@
     return (source == wanted).astype(jnp.bfloat16)
 
 
-def spread_kernel(own, groups, kept, away, ids, out):
+def spread_kernel(groups, kept, away, ids, out):
     coef = kept[...] + away[...]
     here = lax.broadcasted_iota(jnp.int32, ids.shape, 1) == lax.axis_index(CHIPS)
     ell = jnp.sum(jnp.where(here, ids[...], 0), axis=1, keepdims=True)
@@ -30,33 +30,28 @@
     chosen = jnp.where(slot < 2 * ell + 1, coef, 0.0)
     energy = jnp.sum(chosen * coef, axis=0, keepdims=True)
     peak = jnp.max(jnp.abs(chosen), axis=0, keepdims=True)
-    count = out.shape[0] // groups
     width = energy.shape[1]
-    lane = lax.broadcasted_iota(jnp.int32, (count, width), 1)
-    mine = lane // own == lax.broadcasted_iota(jnp.int32, (count, width), 0)
-    energies = jnp.where(mine, energy, 0.0)
-    peaks = jnp.where(mine, peak, 0.0)
-    shift = own
-    while shift < width:
-        energies = energies + pltpu.roll(energies, shift, 1)
-        peaks = peaks + pltpu.roll(peaks, shift, 1)
-        shift *= 2
-    rows = jnp.where(lane < own, energies, peaks)
+    fold = width // 2
+    lane = lax.broadcasted_iota(jnp.int32, energy.shape, 1)
+    low = jnp.where(lane < fold, energy, pltpu.roll(peak, fold, 1))
+    high = jnp.where(lane < fold, pltpu.roll(energy, fold, 1), peak)
+    count = out.shape[0] // groups // 2
     for group in range(groups):
-        out[pl.ds(group * count, count)] = rows
+        out[pl.ds(2 * group * count, count)] = jnp.broadcast_to(low, (count, width))
+        out[pl.ds((2 * group + 1) * count, count)] = jnp.broadcast_to(high, (count, width))
 
 
-def scale_kernel(own, ells, groups, spread, share, crest):
-    values = spread[...]
-    column = jnp.sum(values, axis=0, keepdims=True) + 1e-06
-    top = jnp.max(values, axis=0, keepdims=True) + 1e-06
+def scale_kernel(own, ells, groups, spread, share, crest, turned):
+    column = jnp.sum(spread[...], axis=0, keepdims=True) + 1e-06
+    top = jnp.max(spread[...], axis=0, keepdims=True) + 1e-06
     first = pl.multiple_of(lax.axis_index("ell") * ells, ells)
     held = spread[pl.ds(first, ells)]
+    fold = held.shape[1] // 2
     lane = lax.broadcasted_iota(jnp.int32, held.shape, 1)
-    scaled = jnp.where(lane < own, ells * groups * held / column, held / top)
-    turned = scaled.T
-    share[...] = turned[:own]
-    crest[...] = turned[own : 2 * own]
+    turned[...] = jnp.where(lane < fold, ells * groups * held / column, held / top).T
+    place = lax.rem(lax.axis_index(CHIPS) * own, fold)
+    share[...] = turned[pl.ds(place, own)]
+    crest[...] = turned[pl.ds(place + fold, own)]
 
 
 def per_device(field, projection, ell_ids):
@@ -86,7 +81,7 @@
     away = lax.ppermute(half(other), "core", [(0, 1), (1, 0)])
     kept = lax.optimization_barrier(half(mine))
     both = pl.pallas_call(
-        functools.partial(spread_kernel, own, groups),
+        functools.partial(spread_kernel, groups),
         out_shape=jax.ShapeDtypeStruct((ells * groups, modes // CORES), jnp.float32),
         in_specs=[pl.BlockSpec(memory_space=pltpu.VMEM)] * 3,
         out_specs=pl.BlockSpec(memory_space=pltpu.VMEM),
@@ -99,6 +94,7 @@
         out_shape=(shape, shape),
         in_specs=[pl.BlockSpec(memory_space=pltpu.VMEM)],
         out_specs=(pl.BlockSpec(memory_space=pltpu.VMEM),) * 2,
+        scratch_shapes=[pltpu.VMEM((modes // CORES, ells), jnp.float32)],
         compiler_params=pltpu.CompilerParams(vmem_limit_bytes=SCOPED),
     )(spread)
     return (share.T, crest.T)

time: 51.9 us -> 51.6 us (level)
  no operation moved by 1% of the time
where the time goes in v6:
time: 51.6 us; the launch traced here: 51.4 us
  blocking collectives  43.2 us (84%)
  starting transfers between devices  3.78 us (7%)
  local copies, waits for them, and re-layouts  1.18 us (2%)
  Pallas kernels  0.96 us (2%)
  matrix products  0.81 us (2%)
  waiting for transfers between devices  0.74 us (1%)
  between operations  0.73 us (1%)
    all_to_all x1, blocking collectives, per_device(): got = lax.all_to_all(sent, CHIPS, 0, 0, tiled=True)  23.5 us
    all_to_all x1, blocking collectives, per_device(): spread = lax.all_to_all(both, ('ell', *CHIPS), 0, 0, tiled=True)  19.6 us
    ppermute x1, starting transfers between devices, per_device(): away = lax.ppermute(half(other), 'core', [(0, 1), (1, 0)])  3.78 us
    unnamed x6, local copies, waits for them, and re-layouts  1.18 us
  transfers between devices with their start and end apart: 1, of which 1 were waited for; matrix products, arithmetic and copies ran while one was open for 1% of the time, Pallas kernels for 0%

profile of v6, /device:TPU:1, one launch (start us, length us, event | category | flops | bytes accessed | tf_op | source)
XLA Modules:
  0.0 51.4 jit_solution(7357714282281215324)
XLA Ops:
  0.6 0.0 copy-start.1
  0.7 1.0 %copy.13 = bf16[8,32,256]{2,0,1:T(8,128)(2,1)S(1)} copy(bf16[8,32,256]{2,1,0:T(8,128)(2,1)} %param.4) | data formatting | bytes 262144 | tf_op args[1]
  1.7 0.0 copy-done.1
  1.7 0.2 copy.12
  2.0 23.5 %all_to_all.16 = bf16[32,8,768]{2,1,0:T(8,128)(2,1)S(1)} all-to-all(bf16[32,8,768]{2,1,0:T(8,128)(2,1)S(1)} %pad_maximum_fusion), channel_id=1, replica_groups=mesh['y'=4,'z'=8,'core'=2,'ell'=4] {'y','z'}, dimensions={0} | all-to-all | bytes 786432 | tf_op jit(solution)/shard_map/all_to_all | solution.py:67
  25.5 0.4 fusion.1
  25.9 3.8 %collective-permute-start = (f32[512,128]{1,0:T(8,128)S(1)}, f32[512,128]{1,0:T(8,128)S(1)}, u32[]{:S(2)}, u32[]{:S(2)}) collective-permute-start(f32[512,128]{1,0:T(8,128)S(1)} %fusion.1), channel_id=1, source_target_pairs={{0,4},{4,0},{1,5},{5,1},{2,6},{6,2},{3,7},{7,3},{8,12},{12,8},{9,1... | collective-permute-start | bytes 786440 | tf_op jit(solution)/shard_map/ppermute | solution.py:81
  29.7 0.4 fusion.kept
  30.1 0.0 copy-start
  30.1 0.7 %collective-permute-done.away = f32[512,128]{1,0:T(8,128)S(1)} collective-permute-done((f32[512,128]{1,0:T(8,128)S(1)}, f32[512,128]{1,0:T(8,128)S(1)}, u32[]{:S(2)}, u32[]{:S(2)}) %collective-permute-start) | collective-permute-done | bytes 262176 | tf_op jit(solution)/shard_map/ppermute | solution.py:81
  30.8 0.0 copy-done
  30.8 0.2 shard_map.50
  31.1 19.6 %all_to_all.17 = f32[128,1,128]{2,1,0:T(1,128)S(1)} all-to-all(f32[128,1,128]{2,1,0:T(1,128)S(1)} %bitcast.17), channel_id=1, replica_groups=mesh['y'=4,'z'=8,'core'=2,'ell'=4] {'ell','y','z'}, dimensions={0} | all-to-all | bytes 131072 | tf_op jit(solution)/shard_map/all_to_all | solution.py:90
  50.7 0.7 %shard_map.51 = (f32[4,32]{1,0:T(4,128)}, f32[4,32]{1,0:T(4,128)}) custom-call(f32[128,128]{1,0:T(8,128)S(1)} %bitcast.16), custom_call_target="tpu_custom_call" | custom-call | tf_op jit(solution)/shard_map/pallas_call | solution.py:92
  (5 shorter events, 0.1 us)
Async XLA Ops:
  0.6 1.1 %copy-start.1 = (bf16[8,32,512]{2,1,0:T(8,128)(2,1)S(1)}, bf16[8,32,512]{2,1,0:T(8,128)(2,1)}, u32[]{:S(2)}) copy-start(bf16[8,32,512]{2,1,0:T(8,128)(2,1)} %param.3) | copy-start | bytes 786436
  25.9 4.9 %collective-permute-start = (f32[512,128]{1,0:T(8,128)S(1)}, f32[512,128]{1,0:T(8,128)S(1)}, u32[]{:S(2)}, u32[]{:S(2)}) collective-permute-start(f32[512,128]{1,0:T(8,128)S(1)} %fusion.1), channel_id=1, source_target_pairs={{0,4},{4,0},{1,5},{5,1},{2,6},{6,2},{3,7},{7,3},{8,12},{12,8},{9,1... | collective-permute-start | bytes 786440 | tf_op jit(solution)/shard_map/ppermute | solution.py:81
  30.1 0.8 %copy-start = (s32[32]{0:T(128)S(1)}, s32[32]{0:T(128)}, u32[]{:S(2)}) copy-start(s32[32]{0:T(128)} %param.5) | copy-start | bytes 388

commit v7 on v6

--- a/solution.py
+++ b/solution.py
@@ -1,4 +1,5 @@
 import functools
+import itertools
 
 import jax
 import jax.numpy as jnp
@@ -15,6 +16,20 @@
 WHERE = ("y", "z", "core")
 
 
+def farthest_first(*sizes):
+    def hops(place):
+        return sum(min(at, size - at) for at, size in zip(place, sizes))
+
+    return sorted(itertools.product(*map(range, sizes)), key=hops)[::-1]
+
+
+def turn_of(order, index):
+    turn = jnp.int32(0)
+    for k, member in enumerate(order):
+        turn = jnp.where(index == member, k, turn)
+    return turn
+
+
 def pick(modes, own, core):
     source = lax.broadcasted_iota(jnp.int32, (modes, modes // CORES), 0)
     target = lax.broadcasted_iota(jnp.int32, (modes, modes // CORES), 1)
@@ -22,9 +37,10 @@
     return (source == wanted).astype(jnp.bfloat16)
 
 
-def spread_kernel(groups, kept, away, ids, out):
+def spread_kernel(groups, order, kept, away, ids, out):
     coef = kept[...] + away[...]
-    here = lax.broadcasted_iota(jnp.int32, ids.shape, 1) == lax.axis_index(CHIPS)
+    turn = turn_of(order, lax.axis_index(CHIPS))
+    here = lax.broadcasted_iota(jnp.int32, ids.shape, 1) == turn
     ell = jnp.sum(jnp.where(here, ids[...], 0), axis=1, keepdims=True)
     slot = lax.broadcasted_iota(jnp.int32, coef.shape, 0)
     chosen = jnp.where(slot < 2 * ell + 1, coef, 0.0)
@@ -33,18 +49,25 @@
     width = energy.shape[1]
     fold = width // 2
     lane = lax.broadcasted_iota(jnp.int32, energy.shape, 1)
-    low = jnp.where(lane < fold, energy, pltpu.roll(peak, fold, 1))
-    high = jnp.where(lane < fold, pltpu.roll(energy, fold, 1), peak)
-    count = out.shape[0] // groups // 2
+    halves = (
+        jnp.where(lane < fold, energy, pltpu.roll(peak, fold, 1)),
+        jnp.where(lane < fold, pltpu.roll(energy, fold, 1), peak),
+    )
+    uppers = [2 * chip // len(order) for chip in order]
     for group in range(groups):
-        out[pl.ds(2 * group * count, count)] = jnp.broadcast_to(low, (count, width))
-        out[pl.ds((2 * group + 1) * count, count)] = jnp.broadcast_to(high, (count, width))
+        at = group * len(order)
+        for upper, run in itertools.groupby(uppers):
+            count = len(list(run))
+            out[pl.ds(at, count)] = jnp.broadcast_to(halves[upper], (count, width))
+            at += count
 
 
-def scale_kernel(own, ells, groups, spread, share, crest, turned):
+def scale_kernel(own, order, spread, share, crest, turned):
+    groups = len(order)
+    ells = spread.shape[0] // groups
     column = jnp.sum(spread[...], axis=0, keepdims=True) + 1e-06
     top = jnp.max(spread[...], axis=0, keepdims=True) + 1e-06
-    first = pl.multiple_of(lax.axis_index("ell") * ells, ells)
+    first = pl.multiple_of(turn_of(order, lax.axis_index("ell")) * ells, ells)
     held = spread[pl.ds(first, ells)]
     fold = held.shape[1] // 2
     lane = lax.broadcasted_iota(jnp.int32, held.shape, 1)
@@ -58,13 +81,20 @@
     radii, ells, slots = field.shape
     modes = projection.shape[2]
     groups = lax.axis_size("ell")
+    chips = [y * lax.axis_size("z") + z for y, z in farthest_first(*map(lax.axis_size, CHIPS))]
+    planes = [x for (x,) in farthest_first(groups)]
+    near = [[chip * CORES + c for chip in chips] for c in range(CORES)]
+    wide = [
+        [(chip * CORES + c) * groups + plane for plane in planes for chip in chips]
+        for c in range(CORES)
+    ]
     own = modes // (ells * CORES)
     core = lax.axis_index("core")
     other = pick(modes, own, 1 - core)
     mine = pick(modes, own, core)
     sent = jnp.concatenate([field.transpose(1, 0, 2), projection.transpose(1, 0, 2)], axis=-1)
     sent, other, mine = lax.optimization_barrier((sent, other, mine))
-    got = lax.all_to_all(sent, CHIPS, 0, 0, tiled=True)
+    got = lax.all_to_all(sent, WHERE, 0, 0, tiled=True, axis_index_groups=near)
     got, ell_ids = lax.optimization_barrier((got, ell_ids))
     got = got.reshape(ells * radii, slots + modes)
     values, weights = got[:, :slots], got[:, slots:]
@@ -81,16 +111,18 @@
     away = lax.ppermute(half(other), "core", [(0, 1), (1, 0)])
     kept = lax.optimization_barrier(half(mine))
     both = pl.pallas_call(
-        functools.partial(spread_kernel, groups),
+        functools.partial(spread_kernel, groups, chips),
         out_shape=jax.ShapeDtypeStruct((ells * groups, modes // CORES), jnp.float32),
         in_specs=[pl.BlockSpec(memory_space=pltpu.VMEM)] * 3,
         out_specs=pl.BlockSpec(memory_space=pltpu.VMEM),
         compiler_params=pltpu.CompilerParams(vmem_limit_bytes=SCOPED),
     )(kept, away, ell_ids[None])
-    spread = lax.all_to_all(both, ("ell", *CHIPS), 0, 0, tiled=True)
+    spread = lax.all_to_all(
+        both, (*WHERE, "ell"), 0, 0, tiled=True, axis_index_groups=wide
+    )
     shape = jax.ShapeDtypeStruct((own, ells), jnp.float32)
     share, crest = pl.pallas_call(
-        functools.partial(scale_kernel, own, ells, groups),
+        functools.partial(scale_kernel, own, planes),
         out_shape=(shape, shape),
         in_specs=[pl.BlockSpec(memory_space=pltpu.VMEM)],
         out_specs=(pl.BlockSpec(memory_space=pltpu.VMEM),) * 2,

time: 51.6 us -> 45.4 us (0.88)
  blocking collectives: 43.2 us -> 39.5 us
  starting transfers between devices: 3.78 us -> 1.01 us
    all_to_all x2, blocking collectives: 43.2 us -> 39.5 us  [the longest x1 23.5 us: per_device(): got = lax.all_to_all(sent, WHERE, 0, 0, tiled=True, axis_index_groups=near)]
    ppermute x1, starting transfers between devices: 3.78 us -> 1.01 us  [per_device(): away = lax.ppermute(half(other), 'core', [(0, 1), (1, 0)])]
where the time goes in v7:
time: 45.4 us; the launch traced here: 45.1 us
  blocking collectives  39.5 us (87%)
  local copies, waits for them, and re-layouts  1.18 us (3%)
  starting transfers between devices  1.01 us (2%)
  Pallas kernels  0.98 us (2%)
  matrix products  0.82 us (2%)
  waiting for transfers between devices  0.73 us (2%)
  between operations  0.73 us (2%)
    all_to_all x1, blocking collectives, per_device(): got = lax.all_to_all(sent, WHERE, 0, 0, tiled=True, axis_index_groups=near)  23.5 us
    all_to_all x1, blocking collectives, per_device(): lax.all_to_all(both, (*WHERE, 'ell'), 0, 0, tiled=True, axis_index_groups...  16.1 us
    unnamed x6, local copies, waits for them, and re-layouts  1.18 us
    ppermute x1, starting transfers between devices, per_device(): away = lax.ppermute(half(other), 'core', [(0, 1), (1, 0)])  1.01 us
  transfers between devices with their start and end apart: 1, of which 1 were waited for; matrix products, arithmetic and copies ran while one was open for 1% of the time, Pallas kernels for 0%

profile of v7, /device:TPU:1, one launch (start us, length us, event | category | flops | bytes accessed | tf_op | source)
XLA Modules:
  0.0 45.1 jit_solution(15250921539342800999)
XLA Ops:
  0.6 0.0 copy-start.1
  0.7 1.0 %copy.13 = bf16[8,32,256]{2,0,1:T(8,128)(2,1)S(1)} copy(bf16[8,32,256]{2,1,0:T(8,128)(2,1)} %param.4) | data formatting | bytes 262144 | tf_op args[1]
  1.7 0.0 copy-done.1
  1.7 0.2 copy.12
  2.0 23.5 %all_to_all.16 = bf16[32,8,768]{2,1,0:T(8,128)(2,1)S(1)} all-to-all(bf16[32,8,768]{2,1,0:T(8,128)(2,1)S(1)} %pad_maximum_fusion), channel_id=1, replica_groups={{160,224,168,152,96,232,216,176,144,104,88,32,240,208,184,136,112,80,40..., dimensions={0} | all-to-all | bytes 786432 | tf_op jit(solution)/shard_map/all_to_all | solution.py:97
  25.4 0.4 fusion.1
  25.9 1.0 %collective-permute-start = (f32[512,128]{1,0:T(8,128)S(1)}, f32[512,128]{1,0:T(8,128)S(1)}, u32[]{:S(2)}, u32[]{:S(2)}) collective-permute-start(f32[512,128]{1,0:T(8,128)S(1)} %fusion.1), channel_id=1, source_target_pairs={{0,4},{4,0},{1,5},{5,1},{2,6},{6,2},{3,7},{7,3},{8,12},{12,8},{9,1... | collective-permute-start | bytes 786440 | tf_op jit(solution)/shard_map/ppermute | solution.py:111
  26.9 0.4 fusion.kept
  27.3 0.0 copy-start
  27.3 0.7 %collective-permute-done.away = f32[512,128]{1,0:T(8,128)S(1)} collective-permute-done((f32[512,128]{1,0:T(8,128)S(1)}, f32[512,128]{1,0:T(8,128)S(1)}, u32[]{:S(2)}, u32[]{:S(2)}) %collective-permute-start) | collective-permute-done | bytes 262176 | tf_op jit(solution)/shard_map/ppermute | solution.py:111
  28.0 0.0 copy-done
  28.0 0.3 shard_map.50
  28.3 16.1 %all_to_all.17 = f32[128,1,128]{2,1,0:T(1,128)S(1)} all-to-all(f32[128,1,128]{2,1,0:T(1,128)S(1)} %bitcast.17), channel_id=1, replica_groups={{162,226,170,154,98,234,218,178,146,106,90,34,242,210,186,138,114,82,42..., dimensions={0} | all-to-all | bytes 131072 | tf_op jit(solution)/shard_map/all_to_all | solution.py:120
  44.3 0.7 %shard_map.51 = (f32[4,32]{1,0:T(4,128)}, f32[4,32]{1,0:T(4,128)}) custom-call(f32[128,128]{1,0:T(8,128)S(1)} %bitcast.16), custom_call_target="tpu_custom_call" | custom-call | tf_op jit(solution)/shard_map/pallas_call | solution.py:124
  (5 shorter events, 0.1 us)
Async XLA Ops:
  0.6 1.1 %copy-start.1 = (bf16[8,32,512]{2,1,0:T(8,128)(2,1)S(1)}, bf16[8,32,512]{2,1,0:T(8,128)(2,1)}, u32[]{:S(2)}) copy-start(bf16[8,32,512]{2,1,0:T(8,128)(2,1)} %param.3) | copy-start | bytes 786436
  25.9 2.2 %collective-permute-start = (f32[512,128]{1,0:T(8,128)S(1)}, f32[512,128]{1,0:T(8,128)S(1)}, u32[]{:S(2)}, u32[]{:S(2)}) collective-permute-start(f32[512,128]{1,0:T(8,128)S(1)} %fusion.1), channel_id=1, source_target_pairs={{0,4},{4,0},{1,5},{5,1},{2,6},{6,2},{3,7},{7,3},{8,12},{12,8},{9,1... | collective-permute-start | bytes 786440 | tf_op jit(solution)/shard_map/ppermute | solution.py:111
  27.3 0.7 %copy-start = (s32[32]{0:T(128)S(1)}, s32[32]{0:T(128)}, u32[]{:S(2)}) copy-start(s32[32]{0:T(128)} %param.5) | copy-start | bytes 388

commit v8 on v7

--- a/solution.py
+++ b/solution.py
@@ -12,6 +12,7 @@
 CORES = 2
 CHIPS_Y = 4
 SCOPED = 4 * 2**20
+SUBLANES = 8
 CHIPS = ("y", "z")
 WHERE = ("y", "z", "core")
 
@@ -71,7 +72,8 @@
     held = spread[pl.ds(first, ells)]
     fold = held.shape[1] // 2
     lane = lax.broadcasted_iota(jnp.int32, held.shape, 1)
-    turned[...] = jnp.where(lane < fold, ells * groups * held / column, held / top).T
+    scaled = jnp.where(lane < fold, ells * groups * held / column, held / top)
+    turned[pl.ds(0, 2 * fold)] = scaled.T
     place = lax.rem(lax.axis_index(CHIPS) * own, fold)
     share[...] = turned[pl.ds(place, own)]
     crest[...] = turned[pl.ds(place + fold, own)]
@@ -126,7 +128,7 @@
         out_shape=(shape, shape),
         in_specs=[pl.BlockSpec(memory_space=pltpu.VMEM)],
         out_specs=(pl.BlockSpec(memory_space=pltpu.VMEM),) * 2,
-        scratch_shapes=[pltpu.VMEM((modes // CORES, ells), jnp.float32)],
+        scratch_shapes=[pltpu.VMEM((modes // CORES + SUBLANES, ells), jnp.float32)],
         compiler_params=pltpu.CompilerParams(vmem_limit_bytes=SCOPED),
     )(spread)
     return (share.T, crest.T)

time: 45.4 us -> 45.4 us (level)
  no operation moved by 1% of the time
where the time goes in v8:
time: 45.4 us; the launch traced here: 45.1 us
  blocking collectives  39.5 us (87%)
  local copies, waits for them, and re-layouts  1.18 us (3%)
  starting transfers between devices  1.01 us (2%)
  Pallas kernels  0.98 us (2%)
  matrix products  0.82 us (2%)
  waiting for transfers between devices  0.73 us (2%)
  between operations  0.73 us (2%)
    all_to_all x1, blocking collectives, per_device(): got = lax.all_to_all(sent, WHERE, 0, 0, tiled=True, axis_index_groups=near)  23.5 us
    all_to_all x1, blocking collectives, per_device(): lax.all_to_all(both, (*WHERE, 'ell'), 0, 0, tiled=True, axis_index_groups...  16.1 us
    unnamed x6, local copies, waits for them, and re-layouts  1.18 us
    ppermute x1, starting transfers between devices, per_device(): away = lax.ppermute(half(other), 'core', [(0, 1), (1, 0)])  1.01 us
  transfers between devices with their start and end apart: 1, of which 1 were waited for; matrix products, arithmetic and copies ran while one was open for 1% of the time, Pallas kernels for 0%

profile of v8, /device:TPU:1, one launch (start us, length us, event | category | flops | bytes accessed | tf_op | source)
XLA Modules:
  0.0 45.1 jit_solution(1044483336376897575)
XLA Ops:
  0.6 0.0 copy-start.1
  0.7 1.0 %copy.13 = bf16[8,32,256]{2,0,1:T(8,128)(2,1)S(1)} copy(bf16[8,32,256]{2,1,0:T(8,128)(2,1)} %param.4) | data formatting | bytes 262144 | tf_op args[1]
  1.7 0.0 copy-done.1
  1.7 0.2 copy.12
  2.0 23.5 %all_to_all.16 = bf16[32,8,768]{2,1,0:T(8,128)(2,1)S(1)} all-to-all(bf16[32,8,768]{2,1,0:T(8,128)(2,1)S(1)} %pad_maximum_fusion), channel_id=1, replica_groups={{160,224,168,152,96,232,216,176,144,104,88,32,240,208,184,136,112,80,40..., dimensions={0} | all-to-all | bytes 786432 | tf_op jit(solution)/shard_map/all_to_all | solution.py:99
  25.4 0.4 fusion.1
  25.9 1.0 %collective-permute-start = (f32[512,128]{1,0:T(8,128)S(1)}, f32[512,128]{1,0:T(8,128)S(1)}, u32[]{:S(2)}, u32[]{:S(2)}) collective-permute-start(f32[512,128]{1,0:T(8,128)S(1)} %fusion.1), channel_id=1, source_target_pairs={{0,4},{4,0},{1,5},{5,1},{2,6},{6,2},{3,7},{7,3},{8,12},{12,8},{9,1... | collective-permute-start | bytes 786440 | tf_op jit(solution)/shard_map/ppermute | solution.py:113
  26.9 0.4 fusion.kept
  27.3 0.0 copy-start
  27.3 0.7 %collective-permute-done.away = f32[512,128]{1,0:T(8,128)S(1)} collective-permute-done((f32[512,128]{1,0:T(8,128)S(1)}, f32[512,128]{1,0:T(8,128)S(1)}, u32[]{:S(2)}, u32[]{:S(2)}) %collective-permute-start) | collective-permute-done | bytes 262176 | tf_op jit(solution)/shard_map/ppermute | solution.py:113
  28.0 0.0 copy-done
  28.0 0.3 shard_map.50
  28.3 16.1 %all_to_all.17 = f32[128,1,128]{2,1,0:T(1,128)S(1)} all-to-all(f32[128,1,128]{2,1,0:T(1,128)S(1)} %bitcast.17), channel_id=1, replica_groups={{162,226,170,154,98,234,218,178,146,106,90,34,242,210,186,138,114,82,42..., dimensions={0} | all-to-all | bytes 131072 | tf_op jit(solution)/shard_map/all_to_all | solution.py:122
  44.3 0.7 %shard_map.51 = (f32[4,32]{1,0:T(4,128)}, f32[4,32]{1,0:T(4,128)}) custom-call(f32[128,128]{1,0:T(8,128)S(1)} %bitcast.16), custom_call_target="tpu_custom_call" | custom-call | tf_op jit(solution)/shard_map/pallas_call | solution.py:126
  (5 shorter events, 0.1 us)
Async XLA Ops:
  0.6 1.1 %copy-start.1 = (bf16[8,32,512]{2,1,0:T(8,128)(2,1)S(1)}, bf16[8,32,512]{2,1,0:T(8,128)(2,1)}, u32[]{:S(2)}) copy-start(bf16[8,32,512]{2,1,0:T(8,128)(2,1)} %param.3) | copy-start | bytes 786436
  25.9 2.2 %collective-permute-start = (f32[512,128]{1,0:T(8,128)S(1)}, f32[512,128]{1,0:T(8,128)S(1)}, u32[]{:S(2)}, u32[]{:S(2)}) collective-permute-start(f32[512,128]{1,0:T(8,128)S(1)} %fusion.1), channel_id=1, source_target_pairs={{0,4},{4,0},{1,5},{5,1},{2,6},{6,2},{3,7},{7,3},{8,12},{12,8},{9,1... | collective-permute-start | bytes 786440 | tf_op jit(solution)/shard_map/ppermute | solution.py:113
  27.3 0.7 %copy-start = (s32[32]{0:T(128)S(1)}, s32[32]{0:T(128)}, u32[]{:S(2)}) copy-start(s32[32]{0:T(128)} %param.5) | copy-start | bytes 388

commit v9 on v8

--- a/solution.py
+++ b/solution.py
@@ -66,13 +66,15 @@
 def scale_kernel(own, order, spread, share, crest, turned):
     groups = len(order)
     ells = spread.shape[0] // groups
-    column = jnp.sum(spread[...], axis=0, keepdims=True) + 1e-06
-    top = jnp.max(spread[...], axis=0, keepdims=True) + 1e-06
+    values = spread[...]
+    fold = values.shape[1] // 2
+    lane = lax.broadcasted_iota(jnp.int32, (1, 2 * fold), 1)
+    column = jnp.sum(values, axis=0, keepdims=True)
+    top = jnp.max(values, axis=0, keepdims=True)
+    below = jnp.where(lane < fold, column, top) + 1e-06
+    above = jnp.where(lane < fold, float(ells * groups), 1.0)
     first = pl.multiple_of(turn_of(order, lax.axis_index("ell")) * ells, ells)
-    held = spread[pl.ds(first, ells)]
-    fold = held.shape[1] // 2
-    lane = lax.broadcasted_iota(jnp.int32, held.shape, 1)
-    scaled = jnp.where(lane < fold, ells * groups * held / column, held / top)
+    scaled = above * spread[pl.ds(first, ells)] / below
     turned[pl.ds(0, 2 * fold)] = scaled.T
     place = lax.rem(lax.axis_index(CHIPS) * own, fold)
     share[...] = turned[pl.ds(place, own)]

time: 45.4 us -> 45.4 us (level)
  no operation moved by 1% of the time
where the time goes in v9:
time: 45.4 us; the launch traced here: 45.1 us
  blocking collectives  39.5 us (87%)
  local copies, waits for them, and re-layouts  1.18 us (3%)
  starting transfers between devices  1.01 us (2%)
  Pallas kernels  0.98 us (2%)
  matrix products  0.82 us (2%)
  waiting for transfers between devices  0.73 us (2%)
  between operations  0.73 us (2%)
    all_to_all x1, blocking collectives, per_device(): got = lax.all_to_all(sent, WHERE, 0, 0, tiled=True, axis_index_groups=near)  23.5 us
    all_to_all x1, blocking collectives, per_device(): lax.all_to_all(both, (*WHERE, 'ell'), 0, 0, tiled=True, axis_index_groups...  16.1 us
    unnamed x6, local copies, waits for them, and re-layouts  1.18 us
    ppermute x1, starting transfers between devices, per_device(): away = lax.ppermute(half(other), 'core', [(0, 1), (1, 0)])  1.01 us
  transfers between devices with their start and end apart: 1, of which 1 were waited for; matrix products, arithmetic and copies ran while one was open for 1% of the time, Pallas kernels for 0%

profile of v9, /device:TPU:1, one launch (start us, length us, event | category | flops | bytes accessed | tf_op | source)
XLA Modules:
  0.0 45.1 jit_solution(8520545666905909562)
XLA Ops:
  0.6 0.0 copy-start.1
  0.7 1.0 %copy.13 = bf16[8,32,256]{2,0,1:T(8,128)(2,1)S(1)} copy(bf16[8,32,256]{2,1,0:T(8,128)(2,1)} %param.4) | data formatting | bytes 262144 | tf_op args[1]
  1.7 0.0 copy-done.1
  1.7 0.2 copy.12
  2.0 23.5 %all_to_all.16 = bf16[32,8,768]{2,1,0:T(8,128)(2,1)S(1)} all-to-all(bf16[32,8,768]{2,1,0:T(8,128)(2,1)S(1)} %pad_maximum_fusion), channel_id=1, replica_groups={{160,224,168,152,96,232,216,176,144,104,88,32,240,208,184,136,112,80,40..., dimensions={0} | all-to-all | bytes 786432 | tf_op jit(solution)/shard_map/all_to_all | solution.py:101
  25.4 0.4 fusion.1
  25.9 1.0 %collective-permute-start = (f32[512,128]{1,0:T(8,128)S(1)}, f32[512,128]{1,0:T(8,128)S(1)}, u32[]{:S(2)}, u32[]{:S(2)}) collective-permute-start(f32[512,128]{1,0:T(8,128)S(1)} %fusion.1), channel_id=1, source_target_pairs={{0,4},{4,0},{1,5},{5,1},{2,6},{6,2},{3,7},{7,3},{8,12},{12,8},{9,1... | collective-permute-start | bytes 786440 | tf_op jit(solution)/shard_map/ppermute | solution.py:115
  26.9 0.4 fusion.kept
  27.3 0.0 copy-start
  27.3 0.7 %collective-permute-done.away = f32[512,128]{1,0:T(8,128)S(1)} collective-permute-done((f32[512,128]{1,0:T(8,128)S(1)}, f32[512,128]{1,0:T(8,128)S(1)}, u32[]{:S(2)}, u32[]{:S(2)}) %collective-permute-start) | collective-permute-done | bytes 262176 | tf_op jit(solution)/shard_map/ppermute | solution.py:115
  28.0 0.0 copy-done
  28.0 0.3 shard_map.50
  28.3 16.1 %all_to_all.17 = f32[128,1,128]{2,1,0:T(1,128)S(1)} all-to-all(f32[128,1,128]{2,1,0:T(1,128)S(1)} %bitcast.17), channel_id=1, replica_groups={{162,226,170,154,98,234,218,178,146,106,90,34,242,210,186,138,114,82,42..., dimensions={0} | all-to-all | bytes 131072 | tf_op jit(solution)/shard_map/all_to_all | solution.py:124
  44.3 0.7 %shard_map.51 = (f32[4,32]{1,0:T(4,128)}, f32[4,32]{1,0:T(4,128)}) custom-call(f32[128,128]{1,0:T(8,128)S(1)} %bitcast.16), custom_call_target="tpu_custom_call" | custom-call | tf_op jit(solution)/shard_map/pallas_call | solution.py:128
  (5 shorter events, 0.1 us)
Async XLA Ops:
  0.6 1.1 %copy-start.1 = (bf16[8,32,512]{2,1,0:T(8,128)(2,1)S(1)}, bf16[8,32,512]{2,1,0:T(8,128)(2,1)}, u32[]{:S(2)}) copy-start(bf16[8,32,512]{2,1,0:T(8,128)(2,1)} %param.3) | copy-start | bytes 786436
  25.9 2.2 %collective-permute-start = (f32[512,128]{1,0:T(8,128)S(1)}, f32[512,128]{1,0:T(8,128)S(1)}, u32[]{:S(2)}, u32[]{:S(2)}) collective-permute-start(f32[512,128]{1,0:T(8,128)S(1)} %fusion.1), channel_id=1, source_target_pairs={{0,4},{4,0},{1,5},{5,1},{2,6},{6,2},{3,7},{7,3},{8,12},{12,8},{9,1... | collective-permute-start | bytes 786440 | tf_op jit(solution)/shard_map/ppermute | solution.py:115
  27.3 0.7 %copy-start = (s32[32]{0:T(128)S(1)}, s32[32]{0:T(128)}, u32[]{:S(2)}) copy-start(s32[32]{0:T(128)} %param.5) | copy-start | bytes 388

commit v10 on v8

--- a/solution.py
+++ b/solution.py
@@ -13,6 +13,7 @@
 CHIPS_Y = 4
 SCOPED = 4 * 2**20
 SUBLANES = 8
+LEADER = 2
 CHIPS = ("y", "z")
 WHERE = ("y", "z", "core")
 
@@ -84,6 +85,7 @@
     modes = projection.shape[2]
     groups = lax.axis_size("ell")
     chips = [y * lax.axis_size("z") + z for y, z in farthest_first(*map(lax.axis_size, CHIPS))]
+    chips.insert(0, chips.pop(LEADER))
     planes = [x for (x,) in farthest_first(groups)]
     near = [[chip * CORES + c for chip in chips] for c in range(CORES)]
     wide = [

time: 45.4 us -> 45.5 us (level)
  blocking collectives: 39.5 us -> 38.9 us
  starting transfers between devices: 1.01 us -> 1.59 us
    all_to_all x1, blocking collectives: 23.5 us -> 22.9 us  [per_device(): got = lax.all_to_all(sent, WHERE, 0, 0, tiled=True, axis_index_groups=near)]
    ppermute x1, starting transfers between devices: 1.01 us -> 1.59 us  [per_device(): away = lax.ppermute(half(other), 'core', [(0, 1), (1, 0)])]
where the time goes in v10:
time: 45.5 us; the launch traced here: 45 us
  blocking collectives  38.9 us (85%)
  starting transfers between devices  1.59 us (3%)
  local copies, waits for them, and re-layouts  1.18 us (3%)
  Pallas kernels  0.98 us (2%)
  matrix products  0.82 us (2%)
  waiting for transfers between devices  0.73 us (2%)
  between operations  0.73 us (2%)
    all_to_all x1, blocking collectives, per_device(): got = lax.all_to_all(sent, WHERE, 0, 0, tiled=True, axis_index_groups=near)  22.9 us
    all_to_all x1, blocking collectives, per_device(): lax.all_to_all(both, (*WHERE, 'ell'), 0, 0, tiled=True, axis_index_groups...  16 us
    ppermute x1, starting transfers between devices, per_device(): away = lax.ppermute(half(other), 'core', [(0, 1), (1, 0)])  1.59 us
    unnamed x6, local copies, waits for them, and re-layouts  1.18 us
  transfers between devices with their start and end apart: 1, of which 1 were waited for; matrix products, arithmetic and copies ran while one was open for 1% of the time, Pallas kernels for 0%

profile of v10, /device:TPU:1, one launch (start us, length us, event | category | flops | bytes accessed | tf_op | source)
XLA Modules:
  0.0 45.0 jit_solution(4427477098064124187)
XLA Ops:
  0.6 0.0 copy-start.1
  0.7 1.0 %copy.13 = bf16[8,32,256]{2,0,1:T(8,128)(2,1)S(1)} copy(bf16[8,32,256]{2,1,0:T(8,128)(2,1)} %param.4) | data formatting | bytes 262144 | tf_op args[1]
  1.7 0.0 copy-done.1
  1.7 0.2 copy.12
  2.0 22.9 %all_to_all.16 = bf16[32,8,768]{2,1,0:T(8,128)(2,1)S(1)} all-to-all(bf16[32,8,768]{2,1,0:T(8,128)(2,1)S(1)} %pad_maximum_fusion), channel_id=1, replica_groups={{168,160,224,152,96,232,216,176,144,104,88,32,240,208,184,136,112,80,40..., dimensions={0} | all-to-all | bytes 786432 | tf_op jit(solution)/shard_map/all_to_all | solution.py:101
  24.8 0.4 fusion.1
  25.3 1.6 %collective-permute-start = (f32[512,128]{1,0:T(8,128)S(1)}, f32[512,128]{1,0:T(8,128)S(1)}, u32[]{:S(2)}, u32[]{:S(2)}) collective-permute-start(f32[512,128]{1,0:T(8,128)S(1)} %fusion.1), channel_id=1, source_target_pairs={{0,4},{4,0},{1,5},{5,1},{2,6},{6,2},{3,7},{7,3},{8,12},{12,8},{9,1... | collective-permute-start | bytes 786440 | tf_op jit(solution)/shard_map/ppermute | solution.py:115
  26.9 0.4 fusion.kept
  27.3 0.0 copy-start
  27.3 0.7 %collective-permute-done.away = f32[512,128]{1,0:T(8,128)S(1)} collective-permute-done((f32[512,128]{1,0:T(8,128)S(1)}, f32[512,128]{1,0:T(8,128)S(1)}, u32[]{:S(2)}, u32[]{:S(2)}) %collective-permute-start) | collective-permute-done | bytes 262176 | tf_op jit(solution)/shard_map/ppermute | solution.py:115
  28.0 0.0 copy-done
  28.0 0.3 shard_map.50
  28.3 16.0 %all_to_all.17 = f32[128,1,128]{2,1,0:T(1,128)S(1)} all-to-all(f32[128,1,128]{2,1,0:T(1,128)S(1)} %bitcast.17), channel_id=1, replica_groups={{170,162,226,154,98,234,218,178,146,106,90,34,242,210,186,138,114,82,42..., dimensions={0} | all-to-all | bytes 131072 | tf_op jit(solution)/shard_map/all_to_all | solution.py:124
  44.3 0.7 %shard_map.51 = (f32[4,32]{1,0:T(4,128)}, f32[4,32]{1,0:T(4,128)}) custom-call(f32[128,128]{1,0:T(8,128)S(1)} %bitcast.16), custom_call_target="tpu_custom_call" | custom-call | tf_op jit(solution)/shard_map/pallas_call | solution.py:128
  (5 shorter events, 0.1 us)
Async XLA Ops:
  0.6 1.1 %copy-start.1 = (bf16[8,32,512]{2,1,0:T(8,128)(2,1)S(1)}, bf16[8,32,512]{2,1,0:T(8,128)(2,1)}, u32[]{:S(2)}) copy-start(bf16[8,32,512]{2,1,0:T(8,128)(2,1)} %param.3) | copy-start | bytes 786436
  25.3 2.8 %collective-permute-start = (f32[512,128]{1,0:T(8,128)S(1)}, f32[512,128]{1,0:T(8,128)S(1)}, u32[]{:S(2)}, u32[]{:S(2)}) collective-permute-start(f32[512,128]{1,0:T(8,128)S(1)} %fusion.1), channel_id=1, source_target_pairs={{0,4},{4,0},{1,5},{5,1},{2,6},{6,2},{3,7},{7,3},{8,12},{12,8},{9,1... | collective-permute-start | bytes 786440 | tf_op jit(solution)/shard_map/ppermute | solution.py:115
  27.3 0.7 %copy-start = (s32[32]{0:T(128)S(1)}, s32[32]{0:T(128)}, u32[]{:S(2)}) copy-start(s32[32]{0:T(128)} %param.5) | copy-start | bytes 388

commit v11 on v9

--- a/solution.py
+++ b/solution.py
@@ -13,6 +13,7 @@
 CHIPS_Y = 4
 SCOPED = 4 * 2**20
 SUBLANES = 8
+LEADER = 2
 CHIPS = ("y", "z")
 WHERE = ("y", "z", "core")
 
@@ -86,6 +87,7 @@
     modes = projection.shape[2]
     groups = lax.axis_size("ell")
     chips = [y * lax.axis_size("z") + z for y, z in farthest_first(*map(lax.axis_size, CHIPS))]
+    chips.insert(0, chips.pop(LEADER))
     planes = [x for (x,) in farthest_first(groups)]
     near = [[chip * CORES + c for chip in chips] for c in range(CORES)]
     wide = [

time: 45.4 us -> 45.5 us (level)
  blocking collectives: 39.5 us -> 38.9 us
  starting transfers between devices: 1.01 us -> 1.59 us
    all_to_all x1, blocking collectives: 23.5 us -> 22.9 us  [per_device(): got = lax.all_to_all(sent, WHERE, 0, 0, tiled=True, axis_index_groups=near)]
    ppermute x1, starting transfers between devices: 1.01 us -> 1.59 us  [per_device(): away = lax.ppermute(half(other), 'core', [(0, 1), (1, 0)])]
where the time goes in v11:
time: 45.5 us; the launch traced here: 45 us
  blocking collectives  38.9 us (85%)
  starting transfers between devices  1.59 us (3%)
  local copies, waits for them, and re-layouts  1.18 us (3%)
  Pallas kernels  0.98 us (2%)
  matrix products  0.82 us (2%)
  waiting for transfers between devices  0.73 us (2%)
  between operations  0.73 us (2%)
    all_to_all x1, blocking collectives, per_device(): got = lax.all_to_all(sent, WHERE, 0, 0, tiled=True, axis_index_groups=near)  22.9 us
    all_to_all x1, blocking collectives, per_device(): lax.all_to_all(both, (*WHERE, 'ell'), 0, 0, tiled=True, axis_index_groups...  16 us
    ppermute x1, starting transfers between devices, per_device(): away = lax.ppermute(half(other), 'core', [(0, 1), (1, 0)])  1.59 us
    unnamed x6, local copies, waits for them, and re-layouts  1.18 us
  transfers between devices with their start and end apart: 1, of which 1 were waited for; matrix products, arithmetic and copies ran while one was open for 1% of the time, Pallas kernels for 0%

profile of v11, /device:TPU:1, one launch (start us, length us, event | category | flops | bytes accessed | tf_op | source)
XLA Modules:
  0.0 45.0 jit_solution(5242944757386320594)
XLA Ops:
  0.6 0.0 copy-start.1
  0.7 1.0 %copy.13 = bf16[8,32,256]{2,0,1:T(8,128)(2,1)S(1)} copy(bf16[8,32,256]{2,1,0:T(8,128)(2,1)} %param.4) | data formatting | bytes 262144 | tf_op args[1]
  1.7 0.0 copy-done.1
  1.7 0.2 copy.12
  2.0 22.9 %all_to_all.16 = bf16[32,8,768]{2,1,0:T(8,128)(2,1)S(1)} all-to-all(bf16[32,8,768]{2,1,0:T(8,128)(2,1)S(1)} %pad_maximum_fusion), channel_id=1, replica_groups={{168,160,224,152,96,232,216,176,144,104,88,32,240,208,184,136,112,80,40..., dimensions={0} | all-to-all | bytes 786432 | tf_op jit(solution)/shard_map/all_to_all | solution.py:103
  24.8 0.4 fusion.1
  25.3 1.6 %collective-permute-start = (f32[512,128]{1,0:T(8,128)S(1)}, f32[512,128]{1,0:T(8,128)S(1)}, u32[]{:S(2)}, u32[]{:S(2)}) collective-permute-start(f32[512,128]{1,0:T(8,128)S(1)} %fusion.1), channel_id=1, source_target_pairs={{0,4},{4,0},{1,5},{5,1},{2,6},{6,2},{3,7},{7,3},{8,12},{12,8},{9,1... | collective-permute-start | bytes 786440 | tf_op jit(solution)/shard_map/ppermute | solution.py:117
  26.9 0.4 fusion.kept
  27.3 0.0 copy-start
  27.3 0.7 %collective-permute-done.away = f32[512,128]{1,0:T(8,128)S(1)} collective-permute-done((f32[512,128]{1,0:T(8,128)S(1)}, f32[512,128]{1,0:T(8,128)S(1)}, u32[]{:S(2)}, u32[]{:S(2)}) %collective-permute-start) | collective-permute-done | bytes 262176 | tf_op jit(solution)/shard_map/ppermute | solution.py:117
  28.0 0.0 copy-done
  28.0 0.3 shard_map.50
  28.3 16.0 %all_to_all.17 = f32[128,1,128]{2,1,0:T(1,128)S(1)} all-to-all(f32[128,1,128]{2,1,0:T(1,128)S(1)} %bitcast.17), channel_id=1, replica_groups={{170,162,226,154,98,234,218,178,146,106,90,34,242,210,186,138,114,82,42..., dimensions={0} | all-to-all | bytes 131072 | tf_op jit(solution)/shard_map/all_to_all | solution.py:126
  44.3 0.7 %shard_map.51 = (f32[4,32]{1,0:T(4,128)}, f32[4,32]{1,0:T(4,128)}) custom-call(f32[128,128]{1,0:T(8,128)S(1)} %bitcast.16), custom_call_target="tpu_custom_call" | custom-call | tf_op jit(solution)/shard_map/pallas_call | solution.py:130
  (5 shorter events, 0.1 us)
Async XLA Ops:
  0.6 1.1 %copy-start.1 = (bf16[8,32,512]{2,1,0:T(8,128)(2,1)S(1)}, bf16[8,32,512]{2,1,0:T(8,128)(2,1)}, u32[]{:S(2)}) copy-start(bf16[8,32,512]{2,1,0:T(8,128)(2,1)} %param.3) | copy-start | bytes 786436
  25.3 2.8 %collective-permute-start = (f32[512,128]{1,0:T(8,128)S(1)}, f32[512,128]{1,0:T(8,128)S(1)}, u32[]{:S(2)}, u32[]{:S(2)}) collective-permute-start(f32[512,128]{1,0:T(8,128)S(1)} %fusion.1), channel_id=1, source_target_pairs={{0,4},{4,0},{1,5},{5,1},{2,6},{6,2},{3,7},{7,3},{8,12},{12,8},{9,1... | collective-permute-start | bytes 786440 | tf_op jit(solution)/shard_map/ppermute | solution.py:117
  27.3 0.7 %copy-start = (s32[32]{0:T(128)S(1)}, s32[32]{0:T(128)}, u32[]{:S(2)}) copy-start(s32[32]{0:T(128)} %param.5) | copy-start | bytes 388
